TPU v7x, 256 devices: a 2x2x32 block of a 4x8x32 slice. The times are simulated.
256 devices in a mesh: groups: 4 (over y, x), neuron: 64 (over z, core).
Axes of the slice: x: 2, y: 2, z: 32, core: 2. Of those that a mesh axis runs over, the one named last changes fastest.
The devices are a block of a 4x8x32 slice.
Arguments:
- queries: bfloat16 [2048, 8, 128], P(('groups', 'neuron')), parts along dimension 0, may hold values from -18 to 18
- keys: bfloat16 [2048, 1024, 128], P(('groups', 'neuron')), parts along dimension 0, may hold values from -6 to 6
- values: bfloat16 [2048, 1024, 128], P(('groups', 'neuron')), parts along dimension 0, may hold values from -6 to 6
- lengths: int32 [512], P('groups'), parts along dimension 0, may hold values from 256 to 1024
- active_blocks: int32 [64, 32], P('groups'), parts along dimension 0, may hold values from 0 to 111, all different within a row
- residual: bfloat16 [512, 4096], P('groups', 'neuron'), parts along dimension 0, may hold values from -18 to 18
- out_weight: bfloat16 [4096, 4096], P(None, 'neuron'), may hold values from -0.09375 to 0.09375
- norm_gain: bfloat16 [4096], P('neuron'), may hold values from 0.099609375 to 1.8984375
- gate_weight: bfloat16 [4096, 14336], P('neuron'), may hold values from -0.09375 to 0.09375
- up_weight: bfloat16 [4096, 14336], P('neuron'), may hold values from -0.09375 to 0.09375
- down_weight: bfloat16 [14336, 4096], P(None, 'neuron'), may hold values from -0.09375 to 0.09375
Outputs:
- layer_out: bfloat16 [512, 4096], P('groups', 'neuron'), parts along dimension 0
There are 4 independent parts, one for each index of `groups`. A program takes and returns all parts, laid end to end along the dimension named above; an argument that names none is the same for every part. Nothing has to cross between parts.
Inputs may be any that keep to these rules, and one draw needn't show every extreme that they name: `active_blocks`: each row names 32 different blocks; every block is named by some row.
All inputs are finite; a program needn't handle non-finite values.
Results may differ from a plain program's by a relative error of at most 0.0052.
Values may be sent and summed in bfloat16 or wider, within the bound.
No kernel may reach another device: no remote copies, remote signals or barrier semaphores. Data moves between devices by JAX's collectives and lax.ppermute only.
A program may use at most 64 MiB of HBM per device.

v0:
```python
import functools

import jax
import jax.numpy as jnp
from jax import lax
from jax.sharding import Mesh
from jax.sharding import PartitionSpec as P

D = 4096
BLK = 128
ROWS = 128
NEURON = ("neuron_0", "neuron_1")
GROUPS_NEURON = ("groups", "neuron_0", "neuron_1")


def joined_along(blocks, dim):
    blocks = jnp.moveaxis(blocks, 0, dim)
    lengths = blocks.shape
    return blocks.reshape(*lengths[:dim], lengths[dim] * lengths[dim + 1], *lengths[dim + 2 :])


def stacked_from(x, axes, order):
    blocks = x[None]
    for k in order:
        blocks = lax.all_gather(blocks, axes[k], axis=0, tiled=True)
    held = [lax.axis_size(axes[k]) for k in reversed(order)]
    blocks = blocks.reshape(*held, *x.shape)
    turned = sorted(range(len(order)), key=lambda place: order[len(order) - 1 - place])
    return blocks.transpose(*turned, *range(len(order), blocks.ndim)).reshape(-1, *x.shape)


def gather_axes(x, axes, order, dim):
    return joined_along(stacked_from(x, axes, order), dim)


def over_axes(x, axes):
    return functools.reduce(lax.psum, axes, x)


def in_one_piece(arrays, axis, dim, along):
    ends, at = ([], 0)
    for a in arrays[:-1]:
        at += a.shape[along]
        ends.append(at)
    both = jnp.concatenate(arrays, axis=along)
    return tuple(
        jnp.split(lax.psum_scatter(both, axis, scatter_dimension=dim, tiled=True), ends, axis=along)
    )


def whole_attention(queries, keys, values, live_lengths, score_scale):
    scores = (
        jnp.einsum("egc,etc->egt", queries, keys, preferred_element_type=jnp.float32) * score_scale
    )
    live_mask = (
        jnp.arange(keys.shape[1], dtype=jnp.int32)[None, None, :] < live_lengths[:, None, None]
    )
    scores = jnp.where(live_mask, scores, -1e30)
    running_max = jnp.max(scores, axis=-1, keepdims=True)
    weights = jnp.where(live_mask, jnp.exp(scores - running_max), 0.0)
    probs = (weights / jnp.sum(weights, axis=-1, keepdims=True)).astype(jnp.bfloat16)
    return jnp.einsum("egt,etc->egc", probs, values, preferred_element_type=jnp.float32).astype(
        jnp.bfloat16
    )


def body(
    queries,
    keys,
    values,
    lengths,
    active_blocks,
    residual,
    out_weight,
    norm_gain,
    gate_weight,
    up_weight,
    down_weight,
):
    entries = keys.shape[0]
    first_entry = lax.axis_index(NEURON) * entries
    row_start = first_entry % ROWS
    live_lengths = lax.dynamic_slice_in_dim(lengths, row_start, entries)
    score_scale = queries.shape[2] ** (-0.5)
    attended = whole_attention(queries, keys, values, live_lengths, score_scale)
    attended = attended.reshape(entries, -1)
    gathered = gather_axes(attended, NEURON, (0, 1), 0)
    by_head = gathered.reshape(gathered.shape[0] // ROWS, ROWS, gathered.shape[1])
    out_heads = out_weight.reshape(by_head.shape[0], by_head.shape[2], out_weight.shape[1])
    stream = residual.astype(jnp.float32) + jnp.einsum(
        "hrc,hcd->rd", by_head, out_heads, preferred_element_type=jnp.float32
    )
    square_sums = over_axes(jnp.sum(stream * stream, axis=1), NEURON)
    normed = (
        stream * lax.rsqrt(square_sums / D + 1e-05)[:, None] * norm_gain.astype(jnp.float32)
    ).astype(jnp.bfloat16)
    num_groups = active_blocks.shape[0]
    group_rows = ROWS // num_groups
    local_width = gate_weight.shape[0]
    gate_blocks = gate_weight.reshape(local_width, -1, BLK)
    up_blocks = up_weight.reshape(local_width, -1, BLK)
    down_blocks = down_weight.reshape(-1, BLK, down_weight.shape[1])

    def project_up(operand):
        rows_in, picked = operand
        gate_cols = jnp.take(gate_blocks, picked, axis=1).reshape(local_width, -1)
        up_cols = jnp.take(up_blocks, picked, axis=1).reshape(local_width, -1)
        return (
            jnp.dot(rows_in, gate_cols, preferred_element_type=jnp.float32),
            jnp.dot(rows_in, up_cols, preferred_element_type=jnp.float32),
        )

    gate_part, up_part = lax.map(
        project_up, (normed.reshape(num_groups, group_rows, local_width), active_blocks)
    )
    gate_part = gate_part.reshape(ROWS, -1)
    up_part = up_part.reshape(ROWS, -1)
    gate_share, up_share = in_one_piece((gate_part, up_part), NEURON, 1, 0)
    share_out = (jnp.maximum(gate_share, 0.0) * up_share).astype(jnp.bfloat16)
    activated = gather_axes(share_out, NEURON, (0, 1), 1)

    def project_down(operand):
        rows_in, picked = operand
        down_rows = jnp.take(down_blocks, picked, axis=0).reshape(-1, down_blocks.shape[2])
        return jnp.dot(rows_in, down_rows, preferred_element_type=jnp.float32)

    down_part = lax.map(
        project_down, (activated.reshape(num_groups, group_rows, -1), active_blocks)
    )
    return (stream + down_part.reshape(ROWS, -1)).astype(jnp.bfloat16)


def solution(mesh):
    split = Mesh(
        mesh.devices.reshape(mesh.shape["groups"], 32, 2), ("groups", "neuron_0", "neuron_1")
    )
    return jax.shard_map(
        body,
        mesh=split,
        in_specs=(
            P(GROUPS_NEURON, None, None),
            P(GROUPS_NEURON, None, None),
            P(GROUPS_NEURON, None, None),
            P("groups"),
            P("groups", None),
            P("groups", NEURON),
            P(None, NEURON),
            P(NEURON),
            P(NEURON, None),
            P(NEURON, None),
            P(None, NEURON),
        ),
        out_specs=P("groups", NEURON),
        check_vma=False,
    )
```

profile of v0, /device:TPU:37, one launch (start us, length us, event | category | flops | bytes accessed | tf_op | source)
XLA Modules:
  0.0 689.6 jit_solution(6221972844897320573)
XLA Ops:
  11.8 68.9 %all_gather.12 = bf16[32,8,1024]{2,1,0:T(8,128)(2,1)} all-gather(bf16[1,8,1024]{2,1,0:T(8,128)(2,1)S(1)} %broadcast_in_dim_reshape.3), channel_id=1, replica_groups=mesh['groups'=4,'neuron_0'=32,'neuron_1'=2] {'neuron_0'}, dimensions={0}, use_global_device_ids=true | all-gather | bytes 540672 | tf_op jit(solution)/shard_map/all_gather | solution.py:25
  80.8 4.9 copy_bitcast_fusion
  85.7 26.1 %all-gather.4.cloned.1.call-done = bf16[64,8,1024]{2,1,0:T(8,128)(2,1)} async-done(((bf16[32,8,1024]{2,1,0:T(8,128)(2,1)}), bf16[64,8,1024]{2,1,0:T(8,128)(2,1)}) %all-gather.4.cloned.1.call-update) | async-done | bytes 1048592 | tf_op jit(solution)/shard_map/all_gather | solution.py:25
  113.7 44.2 %psum.14 = f32[128]{0:T(128)S(1)} all-reduce(f32[128]{0:T(128)S(1)} %get-tuple-element.125), channel_id=1, replica_groups=mesh['groups'=4,'neuron_0'=32,'neuron_1'=2] {'neuron_0'}, use_global_device_ids=true, to_apply=%region_3.4 | all-reduce | flops 128 | bytes 1024 | tf_op jit(solution)/shard_map/psum | solution.py:37
  157.9 15.4 %psum.15 = f32[128]{0:T(128)S(1)} all-reduce(f32[128]{0:T(128)S(1)} %psum.14), channel_id=1, replica_groups=mesh['groups'=4,'neuron_0'=32,'neuron_1'=2] {'neuron_1'}, use_global_device_ids=true, to_apply=%region_4.5 | all-reduce | flops 128 | bytes 1024 | tf_op jit(solution)/shard_map/psum | solution.py:37
  173.4 109.8 %while.22 = (s32[]{:T(128)}, f32[16,8,4096]{2,1,0:T(8,128)}, f32[16,8,4096]{2,1,0:T(8,128)}, bf16[16,8,64]{2,1,0:T(8,128)(2,1)S(1)}, s32[16,32]{1,0:T(8,128)}, /...) while((s32[]{:T(128)}, f32[16,8,4096]{2,1,0:T(8,128)}, ...), condition=%wide.region_6.8_spmd, body=%wide.region_5.7_spmd.sunk | while | flops 8914114 | bytes 5516057 | solution.py:113
  174.2 2.1 gather_fusion
  176.3 2.1 gather_fusion.1
  181.0 2.1 gather_fusion
  183.2 2.1 gather_fusion.1
  187.9 2.1 gather_fusion
  190.0 2.1 gather_fusion.1
  194.8 2.1 gather_fusion
  196.9 2.1 gather_fusion.1
  201.6 2.1 gather_fusion
  203.8 2.1 gather_fusion.1
  208.5 2.1 gather_fusion
  210.6 2.1 gather_fusion.1
  215.3 2.1 gather_fusion
  217.5 2.1 gather_fusion.1
  242.7 2.1 gather_fusion
  249.6 2.1 gather_fusion
  283.2 2.9 copy.43
  286.1 2.9 copy.44
  289.0 4.4 pad_maximum_fusion
  293.6 206.9 %reduce-scatter.2.cloned.1.call-done = f32[256,64]{0,1:T(8,128)} async-done(((f32[256,4096]{0,1:T(8,128)}), f32[256,64]{0,1:T(8,128)}) %reduce-scatter.2.cloned.1.call-update) | async-done | bytes 65552 | tf_op jit(solution)/shard_map/reduce_scatter | solution.py:47
  501.3 46.7 %all-gather = bf16[4096,64]{0,1:T(8,128)(2,1)S(1)} all-gather(bf16[128,64]{0,1:T(8,128)(2,1)S(1)} %fusion.27), channel_id=2, replica_groups=mesh['groups'=4,'neuron_0'=32,'neuron_1'=2] {'neuron_0'}, dimensions={0}, use_global_device_ids=true | all-gather | bytes 540672 | tf_op jit(solution)/shard_map/all_gather | solution.py:25
  549.0 4.6 copy.48
  553.6 31.4 %all-gather.6.cloned.1.call-done = bf16[64,128,64]{1,0,2:T(8,128)(2,1)} async-done(((bf16[32,128,64]{1,0,2:T(8,128)(2,1)}), bf16[64,128,64]{1,0,2:T(8,128)(2,1)}) %all-gather.6.cloned.1.call-update) | async-done | bytes 1048592 | tf_op jit(solution)/shard_map/all_gather | solution.py:25
  586.9 3.8 copy.47
  590.7 4.2 reshape_reshape.3
  594.8 87.5 %while.23 = (s32[]{:T(128)}, f32[16,8,64]{2,1,0:T(8,128)S(1)}, bf16[16,8,4096]{2,1,0:T(8,128)(2,1)}, s32[16,32]{1,0:T(8,128)}, bf16[112,128,64]{2,1,0:T(8,128)(2,1)}, /*index=5*/s32[]{:T(128)}) while((s32[]{:T(128)}, f32[16,8,64]{2,1,0:T(8,128)S(1)}, bf16[16,8,4096]{2,1,0:T(8,128)(2,1)}, s32[16,32]{1,0:T(8,128)}, ...), condition=%wide.region_9.11_spmd, body=%wide.region_8.10_spmd.sunk | while | flops 4457762 | bytes 3221261 | solution.py:127
  595.5 2.8 gather_fusion.2
  601.0 2.8 gather_fusion.2
  606.5 2.8 gather_fusion.2
  611.9 2.8 gather_fusion.2
  617.4 2.8 gather_fusion.2
  622.9 2.8 gather_fusion.2
  628.3 2.8 gather_fusion.2
  633.8 2.8 gather_fusion.2
  639.3 2.8 gather_fusion.2
  644.8 2.8 gather_fusion.2
  650.2 2.8 gather_fusion.2
  655.7 2.8 gather_fusion.2
  661.2 2.8 gather_fusion.2
  666.7 2.8 gather_fusion.2
  672.1 2.8 gather_fusion.2
  677.6 2.8 gather_fusion.2
  (209 shorter events, 129.5 us)
Async XLA Ops:
  6.5 1.6 copy-start
  6.6 105.3 %all-gather.4.cloned.1.call-start = ((), (), s32[]{:S(2)}) async-start(), calls=%async_computation.1 | async-start | bytes 1572864 | tf_op jit(solution)/shard_map/all_gather | solution.py:25
  9.7 71.1 %copy-start.3 = (bf16[64]{0:T(256)(128)(2,1)S(1)}, bf16[64]{0:T(256)(128)(2,1)}, u32[]{:S(2)}) copy-start(bf16[64]{0:T(256)(128)(2,1)} %param.24) | copy-start | bytes 388
  80.7 419.8 %reduce-scatter.2.cloned.1.call-start = ((), (), s32[]{:S(2)}) async-start(), calls=%async_computation.2 | async-start | bytes 4259840 | tf_op jit(solution)/shard_map/reduce_scatter | solution.py:47
  85.7 27.4 %copy-start.1 = (bf16[4096,64]{0,1:T(8,128)(2,1)S(1)}, bf16[4096,64]{0,1:T(8,128)(2,1)}, u32[]{:S(2)}) copy-start(bf16[4096,64]{0,1:T(8,128)(2,1)} %param.23) | copy-start | bytes 1572868
  85.7 27.4 %copy-start.2 = (bf16[128,64]{0,1:T(8,128)(2,1)S(1)}, bf16[128,64]{0,1:T(8,128)(2,1)}, u32[]{:S(2)}) copy-start(bf16[128,64]{0,1:T(8,128)(2,1)} %param.22) | copy-start | bytes 49156
  293.5 291.5 %all-gather.6.cloned.1.call-start = ((), (), s32[]{:S(2)}) async-start(), calls=%async_computation.3 | async-start | bytes 1572864 | tf_op jit(solution)/shard_map/all_gather | solution.py:25
Sparse Core Ops, SparseCore 0:
  80.8 30.9 all-gather.3
  293.6 206.8 reduce-scatter.1
  549.1 35.8 all-gather.5
where the time goes:
time: 694 us; the launch traced here: 690 us
  waiting for transfers between devices  265 us (38%)
  blocking collectives  175 us (25%)
  local copies, waits for them, and re-layouts  142 us (20%)
  matrix products  48.3 us (7%)
  other arithmetic  45.1 us (6%)
  between operations  13.2 us (2%)
    reduce_scatter x1, waiting for transfers between devices, in_one_piece(): lax.psum_scatter(both, axis, scatter_dimension=dim, tiled=True)  207 us
    all_gather x2, blocking collectives, stacked_from(): blocks = lax.all_gather(blocks, axes[k], axis=0, tiled=True)  116 us
    psum x2, blocking collectives, over_axes(): return functools.reduce(lax.psum, axes, x)  59.6 us
    all_gather x2, waiting for transfers between devices, stacked_from(): blocks = lax.all_gather(blocks, axes[k], axis=0, tiled=True)  57.5 us
    gather x16, local copies, waits for them, and re-layouts, project_down(): jnp.take(down_blocks, picked, axis=0).reshape(-1, down_blocks.shape[2])  44.6 us
    gather x16, local copies, waits for them, and re-layouts, project_up(): up_cols = jnp.take(up_blocks, picked, axis=1).reshape(local_width, -1)  34.3 us
    gather x16, local copies, waits for them, and re-layouts, project_up(): gate_cols = jnp.take(gate_blocks, picked, axis=1).reshape(local_width, -1)  34.3 us
    dot_general x16, matrix products, project_down(): return jnp.dot(rows_in, down_rows, preferred_element_type=jnp.float32)  17.4 us
  transfers between devices with their start and end apart: 3, of which 3 were waited for; matrix products, arithmetic and copies ran while one was open for 1% of the time, Pallas kernels for 0%

commit v1 on v0

v1 whole, which is shorter than its diff:
```python
import jax
import jax.numpy as jnp
import numpy as np
from jax import lax
from jax.experimental import pallas as pl
from jax.experimental.pallas import tpu as pltpu
from jax.sharding import Mesh
from jax.sharding import PartitionSpec as P

D = 4096
BLK = 128
ROWS = 128
FAR, NEAR = 8, 4
DEVICES = FAR * NEAR * 2
SHARE = 8
LANES = 128
CHUNKS = 7
VMEM_LIMIT = 55 * 1024 * 1024
AXES = ("far", "near", "core")
ALL = ("groups",) + AXES
f32, bf16 = jnp.float32, jnp.bfloat16

NEAR_STEPS = ((0, 0), (1, 1), (2, -2), (-1, -1))
MID_STEPS = ((0, 0), (NEAR, -NEAR))
FAR_STEPS = ((0, 0), (2 * NEAR, 2 * NEAR), (-2 * NEAR, -2 * NEAR), (4 * NEAR, -4 * NEAR))


def moved(n, steps, sign=1):
    z, c = divmod(n, 2)
    return (z + sign * steps[c]) % (FAR * NEAR) * 2 + c


def along_z(x, steps):
    return lax.ppermute(x, AXES, [(n, moved(n, steps)) for n in range(DEVICES)])


def other_core(x):
    return lax.ppermute(x, AXES, [(n, n ^ 1) for n in range(DEVICES)])


def gathered(x):
    mine = lax.all_gather(x, "far", axis=0)
    mine = jnp.stack([mine] + [along_z(mine, steps) for steps in NEAR_STEPS[1:]])
    return mine, other_core(mine)


def arrival(n):
    order = []
    for x in range(2):
        for steps in NEAR_STEPS:
            z, c = divmod(moved(n ^ x, steps, -1), 2)
            order += [(a * NEAR + z % NEAR) * 2 + c for a in range(FAR)]
    return order


def summed(kept, sent):
    kept = kept + other_core(sent).astype(f32)
    sent = kept.astype(bf16)
    got = [along_z(sent[s], NEAR_STEPS[s]) for s in (2, 1, 3)]
    kept = kept[0] + got[0].astype(f32) + got[1].astype(f32) + got[2].astype(f32)
    half = FAR // 2
    on, back = kept[half].astype(bf16), kept[half + 1].astype(bf16)
    for k in range(half - 1, 0, -1):
        on = (along_z(on, (NEAR, -NEAR)).astype(f32) + kept[k]).astype(bf16)
        if k > 1:
            back = (along_z(back, (-NEAR, NEAR)).astype(f32) + kept[FAR + 1 - k]).astype(bf16)
    return kept[0] + along_z(on, (NEAR, -NEAR)).astype(f32) + along_z(back, (-NEAR, NEAR)).astype(f32)


def departure(n):
    return [
        moved(moved(n ^ x, steps), (NEAR * k, -NEAR * k))
        for x in range(2)
        for steps in NEAR_STEPS
        for k in range(FAR)
    ]


def whole_attention(queries, keys, values, live_lengths, score_scale):
    scores = jnp.einsum("egc,etc->egt", queries, keys, preferred_element_type=f32) * score_scale
    live_mask = (
        jnp.arange(keys.shape[1], dtype=jnp.int32)[None, None, :] < live_lengths[:, None, None]
    )
    scores = jnp.where(live_mask, scores, -1e30)
    running_max = jnp.max(scores, axis=-1, keepdims=True)
    weights = jnp.where(live_mask, jnp.exp(scores - running_max), 0.0)
    probs = (weights / jnp.sum(weights, axis=-1, keepdims=True)).astype(bf16)
    return jnp.einsum("egt,etc->egc", probs, values, preferred_element_type=f32).astype(bf16)


def nt_dot(a, b):
    return lax.dot_general(a, b, (((1,), (1,)), ((), ())), preferred_element_type=f32)


def rows_of(g):
    return pl.ds(pl.multiple_of(g * SHARE, SHARE), SHARE)


def up_kernel(
    order, active, mine, theirs, residual, out_t, gain, gate, up,
    stream, kept, sent, heads, squares, gates, ups, both, arrived,
):
    groups = active.shape[0]
    half = DEVICES // 2
    cols = gate.shape[1] // CHUNKS
    copies = []
    for i in range(CHUNKS):
        at = pl.ds(i * cols, cols)
        copies.append([
            pltpu.make_async_copy(gate.at[:, at], gates.at[:, at], arrived.at[0, i]),
            pltpu.make_async_copy(up.at[:, at], ups.at[:, at], arrived.at[1, i]),
        ])
        for copy in copies[-1]:
            copy.start()

    for x, buf in enumerate((mine, theirs)):

        @pl.loop(0, half)
        def _(i):
            device = order[0, x * half + i]
            heads[device // groups, lax.rem(device, groups)] = buf[i].astype(f32)

    width = heads.shape[-1]
    total = residual[...].astype(f32)
    for h in range(heads.shape[0]):
        lhs = heads[h].reshape(ROWS, width).astype(bf16)
        total += nt_dot(lhs, out_t[:, h * width : (h + 1) * width])
    stream[...] = total
    lane = lax.broadcasted_iota(jnp.int32, (ROWS, LANES), 1).astype(f32)
    ones = 1.0 + lane / LANES
    squares[...] = jnp.sum(total * total, axis=1, keepdims=True) * ones
    scaled = total * gain[...]
    high = scaled.astype(bf16)
    low = (scaled - high.astype(f32)).astype(bf16)
    lhs = jnp.concatenate([high, low], axis=1)

    for i in range(CHUNKS):
        for t, w in enumerate((gates, ups)):
            copies[i][t].wait()
            rhs = w[:, i * cols : (i + 1) * cols]
            out = jnp.dot(lhs, jnp.concatenate([rhs, rhs], axis=0), preferred_element_type=f32)
            for j in range(cols // BLK):
                both[i * (cols // BLK) + j, :, t * BLK : (t + 1) * BLK] = out[:, j * BLK : (j + 1) * BLK]

    for x, to in enumerate((kept, sent)):

        @pl.loop(0, half)
        def _(i):
            device = order[1, x * half + i]
            q, g = device // groups, lax.rem(device, groups)
            rows = rows_of(g)
            for j in range(SHARE):
                tile = both[active[g, q * SHARE + j], rows, :].astype(to.dtype)
                to[i, :, j * BLK : (j + 1) * BLK] = tile[:, :BLK]
                to[i, :, (SHARE + j) * BLK : (SHARE + j + 1) * BLK] = tile[:, BLK:]
            to[i, :, 2 * SHARE * BLK :] = squares[rows, :].astype(to.dtype)


def down_kernel(order, active, mine, theirs, stream_t, down_hbm, out_t, dense, down_t, arrived):
    groups = active.shape[0]
    half = DEVICES // 2
    cols = down_t.shape[1] // CHUNKS
    copies = []
    for i in range(CHUNKS):
        at = pl.ds(i * cols, cols)
        copies.append(pltpu.make_async_copy(down_hbm.at[:, at], down_t.at[:, at], arrived.at[i]))
        copies[-1].start()
    dense[...] = jnp.zeros_like(dense)
    for x, buf in enumerate((mine, theirs)):

        @pl.loop(0, half)
        def _(i):
            device = order[0, x * half + i]
            q, g = device // groups, lax.rem(device, groups)
            rows = rows_of(g)
            tile = buf[i].astype(f32)
            for j in range(SHARE):
                dense[active[g, q * SHARE + j], rows, :] = tile[:, j * BLK : (j + 1) * BLK]

    total = stream_t[...]
    per = 4
    for k in range(dense.shape[0] // per):
        if k * per * BLK % cols == 0:
            copies[k * per * BLK // cols].wait()
        rhs = jnp.concatenate([dense[k * per + j].astype(bf16) for j in range(per)], axis=1)
        total += nt_dot(down_t[:, k * per * BLK : (k + 1) * per * BLK], rhs)
    out_t[...] = total.astype(out_t.dtype)


SMEM = pl.BlockSpec(memory_space=pltpu.SMEM)
VMEM = pl.BlockSpec(memory_space=pltpu.VMEM)
HBM = pl.BlockSpec(memory_space=pltpu.HBM)


def body(
    queries,
    keys,
    values,
    lengths,
    active_blocks,
    residual,
    out_weight,
    norm_gain,
    gate_weight,
    up_weight,
    down_weight,
):
    entries = keys.shape[0]
    me = lax.axis_index(AXES)
    tables = np.array([[arrival(n), departure(n)] for n in range(DEVICES)], np.int32)
    order = lax.dynamic_index_in_dim(jnp.asarray(tables), me, keepdims=False)
    live_lengths = lax.dynamic_slice_in_dim(lengths, (me * entries) % ROWS, entries)
    attended = whole_attention(queries, keys, values, live_lengths, queries.shape[2] ** (-0.5))
    mine, theirs = gathered(attended.reshape(entries, -1))

    width = residual.shape[1]
    half = DEVICES // 2
    features = mine.shape[-1]
    share_cols = 2 * SHARE * BLK + LANES
    flat = (half, SHARE, features)
    stream, kept, sent = pl.pallas_call(
        up_kernel,
        in_specs=[SMEM, SMEM, VMEM, VMEM, VMEM, VMEM, VMEM, HBM, HBM],
        out_specs=[VMEM, VMEM, VMEM],
        out_shape=[
            jax.ShapeDtypeStruct((ROWS, width), f32),
            jax.ShapeDtypeStruct((half, SHARE, share_cols), f32),
            jax.ShapeDtypeStruct((half, SHARE, share_cols), bf16),
        ],
        scratch_shapes=[
            pltpu.VMEM((out_weight.shape[0] // features, ROWS // SHARE, SHARE, features), f32),
            pltpu.VMEM((ROWS, LANES), f32),
            pltpu.VMEM(gate_weight.shape, bf16),
            pltpu.VMEM(up_weight.shape, bf16),
            pltpu.VMEM((gate_weight.shape[1] // BLK, ROWS, 2 * BLK), f32),
            pltpu.SemaphoreType.DMA((2, CHUNKS)),
        ],
        compiler_params=pltpu.CompilerParams(vmem_limit_bytes=VMEM_LIMIT),
        name="up_kernel",
    )(
        order,
        active_blocks,
        mine.reshape(flat),
        theirs.reshape(flat),
        residual,
        out_weight.T,
        norm_gain.astype(f32).reshape(1, width),
        gate_weight,
        up_weight,
    )

    terms = (NEAR, FAR, SHARE, share_cols)
    share = summed(kept.reshape(terms), sent.reshape(terms))
    cols = SHARE * BLK
    weights = 1.0 + jnp.arange(LANES, dtype=f32) / LANES
    square_sums = jnp.sum(share[:, 2 * cols :], axis=1, keepdims=True) / jnp.sum(weights)
    inverse = 1.0 / (square_sums / D + 1e-05)
    activated = jnp.maximum(share[:, :cols], 0.0) * share[:, cols : 2 * cols] * inverse
    mine, theirs = gathered(activated.astype(bf16))

    return pl.pallas_call(
        down_kernel,
        in_specs=[SMEM, SMEM, VMEM, VMEM, VMEM, HBM],
        out_specs=VMEM,
        out_shape=jax.ShapeDtypeStruct((width, ROWS), bf16),
        scratch_shapes=[
            pltpu.VMEM((down_weight.shape[0] // BLK, ROWS, BLK), f32),
            pltpu.VMEM((width, down_weight.shape[0]), bf16),
            pltpu.SemaphoreType.DMA((CHUNKS,)),
        ],
        compiler_params=pltpu.CompilerParams(vmem_limit_bytes=VMEM_LIMIT),
        name="down_kernel",
    )(order, active_blocks, mine.reshape(flat), theirs.reshape(flat), stream.T, down_weight.T).T


def solution(mesh):
    split = Mesh(mesh.devices.reshape(mesh.shape["groups"], FAR, NEAR, 2), ALL)
    return jax.shard_map(
        body,
        mesh=split,
        in_specs=(
            P(ALL, None, None),
            P(ALL, None, None),
            P(ALL, None, None),
            P("groups"),
            P("groups", None),
            P("groups", AXES),
            P(None, AXES),
            P(AXES),
            P(AXES, None),
            P(AXES, None),
            P(None, AXES),
        ),
        out_specs=P("groups", AXES),
        check_vma=False,
    )
```

time: 694 us -> 207 us (0.30)
  waiting for transfers between devices: 265 us -> 39.5 us
  local copies, waits for them, and re-layouts: 142 us -> 5.91 us
  blocking collectives: 175 us -> 80.1 us
  starting transfers between devices: 0.13 us -> 54.9 us
  matrix products: 48.3 us -> 3.59 us
  other arithmetic: 45.1 us -> 4.33 us
  Pallas kernels: 0 us -> 18.4 us
  between operations: 13.2 us -> 0.29 us
    reduce_scatter x1 -> x0, waiting for transfers between devices: 207 us -> none  [in_one_piece(): lax.psum_scatter(both, axis, scatter_dimension=dim, tiled=True)]
    gather x48 -> x0, local copies, waits for them, and re-layouts: 113 us -> none  [the longest x16 44.6 us: project_down(): jnp.take(down_blocks, picked, axis=0).reshape(-1, down_blocks.shape[2])]
    psum x2 -> x0, blocking collectives: 59.6 us -> none  [over_axes(): return functools.reduce(lax.psum, axes, x)]
    all_gather x2 -> x0, waiting for transfers between devices: 57.5 us -> none  [stacked_from(): blocks = lax.all_gather(blocks, axes[k], axis=0, tiled=True)]
    ppermute x0 -> x19, starting transfers between devices: none -> 54.9 us  [the longest x16 31.6 us: along_z(): return lax.ppermute(x, AXES, [(n, moved(n, steps)) for n in range(DEVICES)])]
    dot_general x50 -> x1, matrix products: 46.7 us -> 2.06 us  [whole_attention(): jnp.einsum('egt,etc->egc', probs, values, preferred_element_type=f32)]
    ppermute x0 -> x19, waiting for transfers between devices: none -> 39.5 us  [the longest x16 35.8 us: along_z(): return lax.ppermute(x, AXES, [(n, moved(n, steps)) for n in range(DEVICES)])]
    all_gather x2, blocking collectives: 116 us -> 80.1 us  [gathered(): mine = lax.all_gather(x, 'far', axis=0)]
  transfers between devices with their start and end apart: 3 -> 19, of which waited for: 3 -> 15; matrix products, arithmetic and copies ran while one was open for 1% -> 2% of each run, Pallas kernels for 0% -> 0%
where the time goes in v1:
time: 207 us
  blocking collectives  80.1 us (39%)
  starting transfers between devices  54.9 us (27%)
  waiting for transfers between devices  39.5 us (19%)
  Pallas kernels  18.4 us (9%)
  local copies, waits for them, and re-layouts  5.91 us (3%)
  other arithmetic  4.33 us (2%)
  matrix products  3.59 us (2%)
    all_gather x2, blocking collectives, gathered(): mine = lax.all_gather(x, 'far', axis=0)  80.1 us
    ppermute x16, waiting for transfers between devices, along_z(): return lax.ppermute(x, AXES, [(n, moved(n, steps)) for n in range(DEVICES)])  35.8 us
    ppermute x16, starting transfers between devices, along_z(): return lax.ppermute(x, AXES, [(n, moved(n, steps)) for n in range(DEVICES)])  31.6 us
    ppermute x3, starting transfers between devices, other_core(): return lax.ppermute(x, AXES, [(n, n ^ 1) for n in range(DEVICES)])  23.3 us
    pallas_call x1, Pallas kernels, body(): pl.pallas_call(up_kernel, in_specs=[SMEM, SMEM, VMEM, VMEM, VMEM, VMEM, V...  11.8 us
    pallas_call x1, Pallas kernels, body(): pl.pallas_call(down_kernel, in_specs=[SMEM, SMEM, VMEM, VMEM, VMEM, HBM],...  6.69 us
  transfers between devices with their start and end apart: 19, of which 15 were waited for; matrix products, arithmetic and copies ran while one was open for 2% of the time, Pallas kernels for 0%

profile of v1, /device:TPU:37, one launch (start us, length us, event | category | flops | bytes accessed | tf_op | source)
XLA Modules:
  0.0 207.2 jit_solution(1712956119211242000)
XLA Ops:
  0.0 0.9 dynamic_slice.8
  1.0 0.6 copy-done
  1.6 1.5 fusion.26
  3.2 2.1 convolution_convert_fusion
  5.2 50.6 %all_gather.9 = bf16[8,8,1024]{2,1,0:T(8,128)(2,1)S(1)} all-gather(bf16[1,8,1024]{2,1,0:T(8,128)(2,1)S(1)} %all_gather_reshape.3), channel_id=1, replica_groups=mesh['groups'=4,'far'=8,'near'=4,'core'=2] {'far'}, dimensions={0}, use_global_device_ids=true | all-gather | bytes 147456 | tf_op jit(solution)/shard_map/all_gather | solution.py:42
  55.8 2.4 %collective-permute-start.2 = (bf16[8,8,1024]{2,1,0:T(8,128)(2,1)S(1)}, bf16[8,8,1024]{2,1,0:T(8,128)(2,1)S(1)}, u32[]{:S(2)}, u32[]{:S(2)}) collective-permute-start(bf16[8,8,1024]{2,1,0:T(8,128)(2,1)S(1)} %all_gather.9), channel_id=1, source_target_pairs={{0,62},{1,63},{2,0},{3,1},{4,2},{5,3},{6,4},{7,5},{8,6},{9,7},{10,... | collective-permute-start | bytes 393224 | tf_op jit(solution)/shard_map/ppermute | solution.py:34
  58.2 0.8 collective-permute-start.1
  58.9 0.9 collective-permute-start
  59.9 0.4 collective-permute-done.2
  60.3 3.9 %collective-permute-done.1 = bf16[8,8,1024]{2,1,0:T(8,128)(2,1)S(1)} collective-permute-done((bf16[8,8,1024]{2,1,0:T(8,128)(2,1)S(1)}, bf16[8,8,1024]{2,1,0:T(8,128)(2,1)S(1)}, u32[]{:S(2)}, u32[]{:S(2)}) %collective-permute-start.1) | collective-permute-done | bytes 131104 | tf_op jit(solution)/shard_map/ppermute | solution.py:34
  64.3 9.9 %collective-permute-start.3 = (bf16[4,8,8,1024]{3,2,1,0:T(8,128)(2,1)S(1)}, bf16[4,8,8,1024]{3,2,1,0:T(8,128)(2,1)S(1)}, u32[]{:S(2)}, u32[]{:S(2)}) collective-permute-start(bf16[4,8,8,1024]{3,2,1,0:T(8,128)(2,1)S(1)} %pad_maximum_fusion), channel_id=1, source_target_pairs={{0,1},{1,0},{2,3},{3,2},{4,5},{5,4},{6,7},{7,6},{8,9},{9,8},{10,11... | collective-permute-start | bytes 1572872 | tf_op jit(solution)/shard_map/ppermute | solution.py:38
  74.1 0.7 copy.15.residual
  74.9 1.3 dynamic-slice_bitcast_fusion.order
  76.1 0.5 bitcast_convert_fusion.gain
  76.7 0.8 copy-done.3
  77.4 11.8 %up_kernel.1 = (f32[128,64]{1,0:T(8,128)}, f32[32,8,2176]{2,1,0:T(8,128)}, bf16[32,8,2176]{2,1,0:T(8,128)(2,1)}) custom-call(s32[2,64]{1,0:T(2,128)} %dynamic-slice_bitcast_fusion.order, s32[16,32]{1,0:T(8,128)} %active.3, bf16[32,8,1024]{2,1,0:T(8,128)(2,1)} %bitcast.83, bf16[32,8,1024]{2,1,0:T(8,128)(2,1)} %bitcast.87, bf16[128,64]{1,0:T(8,128)(2,1)} %copy.15.residual, ...), custom_call_target="tpu_custom_call" | custom-call | tf_op jit(solution)/shard_map/up_kernel/pallas_call | solution.py:221
  89.4 2.9 %collective-permute-done.4 = bf16[4,8,8,2176]{3,2,1,0:T(8,128)(2,1)S(1)} collective-permute-done((bf16[4,8,8,2176]{3,2,1,0:T(8,128)(2,1)}, bf16[4,8,8,2176]{3,2,1,0:T(8,128)(2,1)S(1)}, u32[]{:S(2)}, u32[]{:S(2)}) %collective-permute-start.4) | collective-permute-done | bytes 1114144 | tf_op jit(solution)/shard_map/ppermute | solution.py:38
  92.3 1.9 fusion.25
  94.3 1.6 collective-permute-start.5
  96.0 0.3 collective-permute-start.7
  96.3 1.2 collective-permute-start.6
  97.4 8.2 %collective-permute-done.5 = bf16[8,8,2176]{2,1,0:T(8,128)(2,1)S(1)} collective-permute-done((bf16[8,8,2176]{2,1,0:T(8,128)(2,1)S(1)}, bf16[8,8,2176]{2,1,0:T(8,128)(2,1)S(1)}, u32[]{:S(2)}, u32[]{:S(2)}) %collective-permute-start.5) | collective-permute-done | bytes 278560 | tf_op jit(solution)/shard_map/ppermute | solution.py:34
  105.6 4.2 %collective-permute-done.7 = bf16[8,8,2176]{2,1,0:T(8,128)(2,1)S(1)} collective-permute-done((bf16[8,8,2176]{2,1,0:T(8,128)(2,1)S(1)}, bf16[8,8,2176]{2,1,0:T(8,128)(2,1)S(1)}, u32[]{:S(2)}, u32[]{:S(2)}) %collective-permute-start.7) | collective-permute-done | bytes 278560 | tf_op jit(solution)/shard_map/ppermute | solution.py:34
  110.0 3.0 %collective-permute-start.8 = (bf16[8,2176]{1,0:T(8,128)(2,1)S(1)}, bf16[8,2176]{1,0:T(8,128)(2,1)S(1)}, u32[]{:S(2)}, u32[]{:S(2)}) collective-permute-start(bf16[8,2176]{1,0:T(8,128)(2,1)S(1)} %get-tuple-element.20), channel_id=1, source_target_pairs={{0,8},{1,57},{2,10},{3,59},{4,12},{5,61},{6,14},{7,63},{8,16},{9,1... | collective-permute-start | bytes 104456 | tf_op jit(solution)/shard_map/ppermute | solution.py:34
  113.0 4.0 %collective-permute-done.8 = bf16[8,2176]{1,0:T(8,128)(2,1)S(1)} collective-permute-done((bf16[8,2176]{1,0:T(8,128)(2,1)S(1)}, bf16[8,2176]{1,0:T(8,128)(2,1)S(1)}, u32[]{:S(2)}, u32[]{:S(2)}) %collective-permute-start.8) | collective-permute-done | bytes 34848 | tf_op jit(solution)/shard_map/ppermute | solution.py:34
  117.0 3.4 %collective-permute-start.9 = (bf16[8,2176]{1,0:T(8,128)(2,1)S(1)}, bf16[8,2176]{1,0:T(8,128)(2,1)S(1)}, u32[]{:S(2)}, u32[]{:S(2)}) collective-permute-start(bf16[8,2176]{1,0:T(8,128)(2,1)S(1)} %fusion.18), channel_id=1, source_target_pairs={{0,8},{1,57},{2,10},{3,59},{4,12},{5,61},{6,14},{7,63},{8,16},{9,1... | collective-permute-start | bytes 104456 | tf_op jit(solution)/shard_map/ppermute | solution.py:34
  120.4 2.1 %collective-permute-start.12 = (bf16[8,2176]{1,0:T(8,128)(2,1)S(1)}, bf16[8,2176]{1,0:T(8,128)(2,1)S(1)}, u32[]{:S(2)}, u32[]{:S(2)}) collective-permute-start(bf16[8,2176]{1,0:T(8,128)(2,1)S(1)} %get-tuple-element.21), channel_id=1, source_target_pairs={{0,56},{1,9},{2,58},{3,11},{4,60},{5,13},{6,62},{7,15},{8,0},{9,17... | collective-permute-start | bytes 104456 | tf_op jit(solution)/shard_map/ppermute | solution.py:34
  122.5 1.3 collective-permute-done.9
  123.8 3.5 %collective-permute-start.10 = (bf16[8,2176]{1,0:T(8,128)(2,1)S(1)}, bf16[8,2176]{1,0:T(8,128)(2,1)S(1)}, u32[]{:S(2)}, u32[]{:S(2)}) collective-permute-start(bf16[8,2176]{1,0:T(8,128)(2,1)S(1)} %fusion.16), channel_id=1, source_target_pairs={{0,8},{1,57},{2,10},{3,59},{4,12},{5,61},{6,14},{7,63},{8,16},{9,1... | collective-permute-start | bytes 104456 | tf_op jit(solution)/shard_map/ppermute | solution.py:34
  127.4 1.2 collective-permute-done.12
  128.6 3.4 %collective-permute-done.10 = bf16[8,2176]{1,0:T(8,128)(2,1)S(1)} collective-permute-done((bf16[8,2176]{1,0:T(8,128)(2,1)S(1)}, bf16[8,2176]{1,0:T(8,128)(2,1)S(1)}, u32[]{:S(2)}, u32[]{:S(2)}) %collective-permute-start.10) | collective-permute-done | bytes 34848 | tf_op jit(solution)/shard_map/ppermute | solution.py:34
  132.1 2.5 %collective-permute-start.13 = (bf16[8,2176]{1,0:T(8,128)(2,1)S(1)}, bf16[8,2176]{1,0:T(8,128)(2,1)S(1)}, u32[]{:S(2)}, u32[]{:S(2)}) collective-permute-start(bf16[8,2176]{1,0:T(8,128)(2,1)S(1)} %get-tuple-element.19), channel_id=1, source_target_pairs={{0,56},{1,9},{2,58},{3,11},{4,60},{5,13},{6,62},{7,15},{8,0},{9,17... | collective-permute-start | bytes 104456 | tf_op jit(solution)/shard_map/ppermute | solution.py:34
  134.6 3.0 %collective-permute-start.11 = (bf16[8,2176]{1,0:T(8,128)(2,1)S(1)}, bf16[8,2176]{1,0:T(8,128)(2,1)S(1)}, u32[]{:S(2)}, u32[]{:S(2)}) collective-permute-start(bf16[8,2176]{1,0:T(8,128)(2,1)S(1)} %get-tuple-element.18), channel_id=1, source_target_pairs={{0,8},{1,57},{2,10},{3,59},{4,12},{5,61},{6,14},{7,63},{8,16},{9,1... | collective-permute-start | bytes 104456 | tf_op jit(solution)/shard_map/ppermute | solution.py:34
  137.6 1.3 collective-permute-done.13
  138.9 3.2 %collective-permute-start.14 = (bf16[8,2176]{1,0:T(8,128)(2,1)S(1)}, bf16[8,2176]{1,0:T(8,128)(2,1)S(1)}, u32[]{:S(2)}, u32[]{:S(2)}) collective-permute-start(bf16[8,2176]{1,0:T(8,128)(2,1)S(1)} %fusion.10), channel_id=1, source_target_pairs={{0,56},{1,9},{2,58},{3,11},{4,60},{5,13},{6,62},{7,15},{8,0},{9,17... | collective-permute-start | bytes 104456 | tf_op jit(solution)/shard_map/ppermute | solution.py:34
  142.1 0.6 add_reduce_fusion
  142.7 3.4 %collective-permute-done.14 = bf16[8,2176]{1,0:T(8,128)(2,1)S(1)} collective-permute-done((bf16[8,2176]{1,0:T(8,128)(2,1)S(1)}, bf16[8,2176]{1,0:T(8,128)(2,1)S(1)}, u32[]{:S(2)}, u32[]{:S(2)}) %collective-permute-start.14) | collective-permute-done | bytes 34848 | tf_op jit(solution)/shard_map/ppermute | solution.py:34
  146.2 0.7 add_divide_fusion
  147.0 29.6 %all-gather = bf16[64,1024]{1,0:T(8,128)(2,1)S(1)} all-gather(bf16[8,1024]{1,0:T(8,128)(2,1)S(1)} %fusion.22), channel_id=2, replica_groups=mesh['groups'=4,'far'=8,'near'=4,'core'=2] {'far'}, dimensions={0}, use_global_device_ids=true | all-gather | bytes 147456 | tf_op jit(solution)/shard_map/all_gather | solution.py:42
  176.7 3.6 %collective-permute-start.15 = (bf16[8,8,1024]{2,1,0:T(8,128)(2,1)S(1)}, bf16[8,8,1024]{2,1,0:T(8,128)(2,1)S(1)}, u32[]{:S(2)}, u32[]{:S(2)}) collective-permute-start(bf16[8,8,1024]{2,1,0:T(8,128)(2,1)S(1)} %bitcast.91), channel_id=1, source_target_pairs={{0,2},{1,3},{2,4},{3,5},{4,6},{5,7},{6,8},{7,9},{8,10},{9,11},{10,... | collective-permute-start | bytes 393224 | tf_op jit(solution)/shard_map/ppermute | solution.py:34
  180.3 1.1 collective-permute-done.16
  181.4 0.8 collective-permute-done.15
  182.2 2.4 %collective-permute-done.17 = bf16[8,8,1024]{2,1,0:T(8,128)(2,1)S(1)} collective-permute-done((bf16[8,8,1024]{2,1,0:T(8,128)(2,1)S(1)}, bf16[8,8,1024]{2,1,0:T(8,128)(2,1)S(1)}, u32[]{:S(2)}, u32[]{:S(2)}) %collective-permute-start.17) | collective-permute-done | bytes 131104 | tf_op jit(solution)/shard_map/ppermute | solution.py:34
  184.7 13.3 %collective-permute-start.18 = (bf16[4,8,8,1024]{3,2,1,0:T(8,128)(2,1)S(1)}, bf16[4,8,8,1024]{3,2,1,0:T(8,128)(2,1)S(1)}, u32[]{:S(2)}, u32[]{:S(2)}) collective-permute-start(bf16[4,8,8,1024]{3,2,1,0:T(8,128)(2,1)S(1)} %pad_maximum_fusion.1), channel_id=1, source_target_pairs={{0,1},{1,0},{2,3},{3,2},{4,5},{5,4},{6,7},{7,6},{8,9},{9,8},{10,11... | collective-permute-start | bytes 1572872 | tf_op jit(solution)/shard_map/ppermute | solution.py:38
  198.0 0.7 copy.16
  198.7 0.8 collective-permute-done.18
  199.5 0.8 copy-done.4
  200.3 6.7 %down_kernel.1 = bf16[64,128]{1,0:T(8,128)(2,1)} custom-call(s32[2,64]{1,0:T(2,128)} %dynamic-slice_bitcast_fusion.order, s32[16,32]{1,0:T(8,128)} %active.3, bf16[32,8,1024]{2,1,0:T(8,128)(2,1)} %bitcast.84, bf16[32,8,1024]{2,1,0:T(8,128)(2,1)} %bitcast.88, f32[64,128]{1,0:T(8,128)} %bitcast.94, bf16[64,14336]{1,0:T(8,128)(2,1)} %bitcast.85), custom_call_target="tpu_custom_call" | custom-call | tf_op jit(solution)/shard_map/down_kernel/pallas_call | solution.py:261
  (34 shorter events, 1.0 us)
Async XLA Ops:
  0.0 1.6 copy-start
  3.1 71.0 %copy-start.6 = (bf16[128,64]{0,1:T(8,128)(2,1)S(1)}, bf16[128,64]{0,1:T(8,128)(2,1)}, u32[]{:S(2)}) copy-start(bf16[128,64]{0,1:T(8,128)(2,1)} %param.17) | copy-start | bytes 49156
  3.1 73.0 %copy-start.7 = (bf16[64]{0:T(256)(128)(2,1)S(1)}, bf16[64]{0:T(256)(128)(2,1)}, u32[]{:S(2)}) copy-start(bf16[64]{0:T(256)(128)(2,1)} %param.19) | copy-start | bytes 388
  55.8 4.4 %collective-permute-start.2 = (bf16[8,8,1024]{2,1,0:T(8,128)(2,1)S(1)}, bf16[8,8,1024]{2,1,0:T(8,128)(2,1)S(1)}, u32[]{:S(2)}, u32[]{:S(2)}) collective-permute-start(bf16[8,8,1024]{2,1,0:T(8,128)(2,1)S(1)} %all_gather.9), channel_id=1, source_target_pairs={{0,62},{1,63},{2,0},{3,1},{4,2},{5,3},{6,4},{7,5},{8,6},{9,7},{10,... | collective-permute-start | bytes 393224 | tf_op jit(solution)/shard_map/ppermute | solution.py:34
  58.2 6.0 %collective-permute-start.1 = (bf16[8,8,1024]{2,1,0:T(8,128)(2,1)S(1)}, bf16[8,8,1024]{2,1,0:T(8,128)(2,1)S(1)}, u32[]{:S(2)}, u32[]{:S(2)}) collective-permute-start(bf16[8,8,1024]{2,1,0:T(8,128)(2,1)S(1)} %all_gather.9), channel_id=1, source_target_pairs={{0,4},{1,61},{2,6},{3,63},{4,8},{5,1},{6,10},{7,3},{8,12},{9,5},{1... | collective-permute-start | bytes 393224 | tf_op jit(solution)/shard_map/ppermute | solution.py:34
  58.9 5.3 %collective-permute-start = (bf16[8,8,1024]{2,1,0:T(8,128)(2,1)S(1)}, bf16[8,8,1024]{2,1,0:T(8,128)(2,1)S(1)}, u32[]{:S(2)}, u32[]{:S(2)}) collective-permute-start(bf16[8,8,1024]{2,1,0:T(8,128)(2,1)S(1)} %all_gather.9), channel_id=1, source_target_pairs={{0,2},{1,3},{2,4},{3,5},{4,6},{5,7},{6,8},{7,9},{8,10},{9,11},{10,... | collective-permute-start | bytes 393224 | tf_op jit(solution)/shard_map/ppermute | solution.py:34
  64.3 12.4 %copy-start.1 = (bf16[4,8,8,1024]{3,2,1,0:T(8,128)(2,1)}, bf16[4,8,8,1024]{3,2,1,0:T(8,128)(2,1)S(1)}, u32[]{:S(2)}) copy-start(bf16[4,8,8,1024]{3,2,1,0:T(8,128)(2,1)S(1)} %pad_maximum_fusion) | copy-start | bytes 1572868
  64.3 12.4 %collective-permute-start.3 = (bf16[4,8,8,1024]{3,2,1,0:T(8,128)(2,1)S(1)}, bf16[4,8,8,1024]{3,2,1,0:T(8,128)(2,1)S(1)}, u32[]{:S(2)}, u32[]{:S(2)}) collective-permute-start(bf16[4,8,8,1024]{3,2,1,0:T(8,128)(2,1)S(1)} %pad_maximum_fusion), channel_id=1, source_target_pairs={{0,1},{1,0},{2,3},{3,2},{4,5},{5,4},{6,7},{7,6},{8,9},{9,8},{10,11... | collective-permute-start | bytes 1572872 | tf_op jit(solution)/shard_map/ppermute | solution.py:38
  76.6 0.8 copy-start.3
  89.2 3.1 %collective-permute-start.4 = (bf16[4,8,8,2176]{3,2,1,0:T(8,128)(2,1)}, bf16[4,8,8,2176]{3,2,1,0:T(8,128)(2,1)S(1)}, u32[]{:S(2)}, u32[]{:S(2)}) collective-permute-start(bf16[4,8,8,2176]{3,2,1,0:T(8,128)(2,1)} %bitcast.101), channel_id=1, source_target_pairs={{0,1},{1,0},{2,3},{3,2},{4,5},{5,4},{6,7},{7,6},{8,9},{9,8},{10,11... | collective-permute-start | bytes 3342344 | tf_op jit(solution)/shard_map/ppermute | solution.py:38
  94.3 11.3 %collective-permute-start.5 = (bf16[8,8,2176]{2,1,0:T(8,128)(2,1)S(1)}, bf16[8,8,2176]{2,1,0:T(8,128)(2,1)S(1)}, u32[]{:S(2)}, u32[]{:S(2)}) collective-permute-start(bf16[8,8,2176]{2,1,0:T(8,128)(2,1)S(1)} %get-tuple-element.15), channel_id=1, source_target_pairs={{0,4},{1,61},{2,6},{3,63},{4,8},{5,1},{6,10},{7,3},{8,12},{9,5},{1... | collective-permute-start | bytes 835592 | tf_op jit(solution)/shard_map/ppermute | solution.py:34
  96.0 13.9 %collective-permute-start.7 = (bf16[8,8,2176]{2,1,0:T(8,128)(2,1)S(1)}, bf16[8,8,2176]{2,1,0:T(8,128)(2,1)S(1)}, u32[]{:S(2)}, u32[]{:S(2)}) collective-permute-start(bf16[8,8,2176]{2,1,0:T(8,128)(2,1)S(1)} %get-tuple-element.16), channel_id=1, source_target_pairs={{0,62},{1,63},{2,0},{3,1},{4,2},{5,3},{6,4},{7,5},{8,6},{9,7},{10,... | collective-permute-start | bytes 835592 | tf_op jit(solution)/shard_map/ppermute | solution.py:34
  96.3 13.6 %collective-permute-start.6 = (bf16[8,8,2176]{2,1,0:T(8,128)(2,1)S(1)}, bf16[8,8,2176]{2,1,0:T(8,128)(2,1)S(1)}, u32[]{:S(2)}, u32[]{:S(2)}) collective-permute-start(bf16[8,8,2176]{2,1,0:T(8,128)(2,1)S(1)} %get-tuple-element.17), channel_id=1, source_target_pairs={{0,2},{1,3},{2,4},{3,5},{4,6},{5,7},{6,8},{7,9},{8,10},{9,11},{10,... | collective-permute-start | bytes 835592 | tf_op jit(solution)/shard_map/ppermute | solution.py:34
  109.8 88.1 %copy-start.5 = (f32[128,64]{1,0:T(8,128)S(1)}, f32[128,64]{1,0:T(8,128)}, u32[]{:S(2)}) copy-start(f32[128,64]{1,0:T(8,128)} %get-tuple-element.10) | copy-start | bytes 98308
  110.0 7.0 %collective-permute-start.8 = (bf16[8,2176]{1,0:T(8,128)(2,1)S(1)}, bf16[8,2176]{1,0:T(8,128)(2,1)S(1)}, u32[]{:S(2)}, u32[]{:S(2)}) collective-permute-start(bf16[8,2176]{1,0:T(8,128)(2,1)S(1)} %get-tuple-element.20), channel_id=1, source_target_pairs={{0,8},{1,57},{2,10},{3,59},{4,12},{5,61},{6,14},{7,63},{8,16},{9,1... | collective-permute-start | bytes 104456 | tf_op jit(solution)/shard_map/ppermute | solution.py:34
  117.0 6.8 %collective-permute-start.9 = (bf16[8,2176]{1,0:T(8,128)(2,1)S(1)}, bf16[8,2176]{1,0:T(8,128)(2,1)S(1)}, u32[]{:S(2)}, u32[]{:S(2)}) collective-permute-start(bf16[8,2176]{1,0:T(8,128)(2,1)S(1)} %fusion.18), channel_id=1, source_target_pairs={{0,8},{1,57},{2,10},{3,59},{4,12},{5,61},{6,14},{7,63},{8,16},{9,1... | collective-permute-start | bytes 104456 | tf_op jit(solution)/shard_map/ppermute | solution.py:34
  120.4 8.2 %collective-permute-start.12 = (bf16[8,2176]{1,0:T(8,128)(2,1)S(1)}, bf16[8,2176]{1,0:T(8,128)(2,1)S(1)}, u32[]{:S(2)}, u32[]{:S(2)}) collective-permute-start(bf16[8,2176]{1,0:T(8,128)(2,1)S(1)} %get-tuple-element.21), channel_id=1, source_target_pairs={{0,56},{1,9},{2,58},{3,11},{4,60},{5,13},{6,62},{7,15},{8,0},{9,17... | collective-permute-start | bytes 104456 | tf_op jit(solution)/shard_map/ppermute | solution.py:34
  123.8 8.2 %collective-permute-start.10 = (bf16[8,2176]{1,0:T(8,128)(2,1)S(1)}, bf16[8,2176]{1,0:T(8,128)(2,1)S(1)}, u32[]{:S(2)}, u32[]{:S(2)}) collective-permute-start(bf16[8,2176]{1,0:T(8,128)(2,1)S(1)} %fusion.16), channel_id=1, source_target_pairs={{0,8},{1,57},{2,10},{3,59},{4,12},{5,61},{6,14},{7,63},{8,16},{9,1... | collective-permute-start | bytes 104456 | tf_op jit(solution)/shard_map/ppermute | solution.py:34
  132.1 6.8 %collective-permute-start.13 = (bf16[8,2176]{1,0:T(8,128)(2,1)S(1)}, bf16[8,2176]{1,0:T(8,128)(2,1)S(1)}, u32[]{:S(2)}, u32[]{:S(2)}) collective-permute-start(bf16[8,2176]{1,0:T(8,128)(2,1)S(1)} %get-tuple-element.19), channel_id=1, source_target_pairs={{0,56},{1,9},{2,58},{3,11},{4,60},{5,13},{6,62},{7,15},{8,0},{9,17... | collective-permute-start | bytes 104456 | tf_op jit(solution)/shard_map/ppermute | solution.py:34
  134.6 8.2 %collective-permute-start.11 = (bf16[8,2176]{1,0:T(8,128)(2,1)S(1)}, bf16[8,2176]{1,0:T(8,128)(2,1)S(1)}, u32[]{:S(2)}, u32[]{:S(2)}) collective-permute-start(bf16[8,2176]{1,0:T(8,128)(2,1)S(1)} %get-tuple-element.18), channel_id=1, source_target_pairs={{0,8},{1,57},{2,10},{3,59},{4,12},{5,61},{6,14},{7,63},{8,16},{9,1... | collective-permute-start | bytes 104456 | tf_op jit(solution)/shard_map/ppermute | solution.py:34
  138.9 7.2 %collective-permute-start.14 = (bf16[8,2176]{1,0:T(8,128)(2,1)S(1)}, bf16[8,2176]{1,0:T(8,128)(2,1)S(1)}, u32[]{:S(2)}, u32[]{:S(2)}) collective-permute-start(bf16[8,2176]{1,0:T(8,128)(2,1)S(1)} %fusion.10), channel_id=1, source_target_pairs={{0,56},{1,9},{2,58},{3,11},{4,60},{5,13},{6,62},{7,15},{8,0},{9,17... | collective-permute-start | bytes 104456 | tf_op jit(solution)/shard_map/ppermute | solution.py:34
  176.5 4.9 %collective-permute-start.16 = (bf16[8,8,1024]{2,1,0:T(8,128)(2,1)S(1)}, bf16[8,8,1024]{2,1,0:T(8,128)(2,1)S(1)}, u32[]{:S(2)}, u32[]{:S(2)}) collective-permute-start(bf16[8,8,1024]{2,1,0:T(8,128)(2,1)S(1)} %bitcast.90), channel_id=1, source_target_pairs={{0,4},{1,61},{2,6},{3,63},{4,8},{5,1},{6,10},{7,3},{8,12},{9,5},{1... | collective-permute-start | bytes 393224 | tf_op jit(solution)/shard_map/ppermute | solution.py:34
  176.7 5.6 %collective-permute-start.15 = (bf16[8,8,1024]{2,1,0:T(8,128)(2,1)S(1)}, bf16[8,8,1024]{2,1,0:T(8,128)(2,1)S(1)}, u32[]{:S(2)}, u32[]{:S(2)}) collective-permute-start(bf16[8,8,1024]{2,1,0:T(8,128)(2,1)S(1)} %bitcast.91), channel_id=1, source_target_pairs={{0,2},{1,3},{2,4},{3,5},{4,6},{5,7},{6,8},{7,9},{8,10},{9,11},{10,... | collective-permute-start | bytes 393224 | tf_op jit(solution)/shard_map/ppermute | solution.py:34
  180.3 4.3 %collective-permute-start.17 = (bf16[8,8,1024]{2,1,0:T(8,128)(2,1)S(1)}, bf16[8,8,1024]{2,1,0:T(8,128)(2,1)S(1)}, u32[]{:S(2)}, u32[]{:S(2)}) collective-permute-start(bf16[8,8,1024]{2,1,0:T(8,128)(2,1)S(1)} %bitcast.92), channel_id=1, source_target_pairs={{0,62},{1,63},{2,0},{3,1},{4,2},{5,3},{6,4},{7,5},{8,6},{9,7},{10,... | collective-permute-start | bytes 393224 | tf_op jit(solution)/shard_map/ppermute | solution.py:34
  184.7 14.8 %copy-start.2 = (bf16[4,8,8,1024]{3,2,1,0:T(8,128)(2,1)}, bf16[4,8,8,1024]{3,2,1,0:T(8,128)(2,1)S(1)}, u32[]{:S(2)}) copy-start(bf16[4,8,8,1024]{3,2,1,0:T(8,128)(2,1)S(1)} %pad_maximum_fusion.1) | copy-start | bytes 1572868
  184.7 14.8 %collective-permute-start.18 = (bf16[4,8,8,1024]{3,2,1,0:T(8,128)(2,1)S(1)}, bf16[4,8,8,1024]{3,2,1,0:T(8,128)(2,1)S(1)}, u32[]{:S(2)}, u32[]{:S(2)}) collective-permute-start(bf16[4,8,8,1024]{3,2,1,0:T(8,128)(2,1)S(1)} %pad_maximum_fusion.1), channel_id=1, source_target_pairs={{0,1},{1,0},{2,3},{3,2},{4,5},{5,4},{6,7},{7,6},{8,9},{9,8},{10,11... | collective-permute-start | bytes 1572872 | tf_op jit(solution)/shard_map/ppermute | solution.py:38
  199.5 0.8 copy-start.4

commit v2 on v1

--- a/solution.py
+++ b/solution.py
@@ -20,60 +20,82 @@
 ALL = ("groups",) + AXES
 f32, bf16 = jnp.float32, jnp.bfloat16
 
-NEAR_STEPS = ((0, 0), (1, 1), (2, -2), (-1, -1))
-MID_STEPS = ((0, 0), (NEAR, -NEAR))
-FAR_STEPS = ((0, 0), (2 * NEAR, 2 * NEAR), (-2 * NEAR, -2 * NEAR), (4 * NEAR, -4 * NEAR))
-
-
-def moved(n, steps, sign=1):
-    z, c = divmod(n, 2)
-    return (z + sign * steps[c]) % (FAR * NEAR) * 2 + c
-
-
-def along_z(x, steps):
-    return lax.ppermute(x, AXES, [(n, moved(n, steps)) for n in range(DEVICES)])
+SENSE = (-1, 1)
+STEPS = ((0, 1, 2, 3), (4, 1, 2, 3))
+TWO_AWAY = ((1, slice(2, 4)), (-1, slice(1, 3)))
+
+
+def along_z(x, steps, cores=(0, 1)):
+    chips = FAR * NEAR
+    pairs = [(2 * z + c, (z + steps[c]) % chips * 2 + c) for z in range(chips) for c in cores]
+    return lax.ppermute(x, AXES, pairs)
+
+
+def passed_on(x, cores=(0, 1)):
+    return along_z(x, (-NEAR, NEAR), cores)
+
+
+def two_away(x):
+    return [along_z(x[part], (-2 * way, 2 * way)) for way, part in TWO_AWAY]
 
 
 def other_core(x):
-    return lax.ppermute(x, AXES, [(n, n ^ 1) for n in range(DEVICES)])
-
-
-def gathered(x):
-    mine = lax.all_gather(x, "far", axis=0)
-    mine = jnp.stack([mine] + [along_z(mine, steps) for steps in NEAR_STEPS[1:]])
-    return mine, other_core(mine)
+    return lax.ppermute(x, "core", [(0, 1), (1, 0)])
+
+
+def of_core(first, second):
+    return jnp.where(lax.axis_index("core") == 0, first, second)
+
+
+def gathered(pair):
+    held = [pair]
+    for k in range(3):
+        held.append(passed_on(held[-1]))
+    held[0] = of_core(pair, passed_on(held[-1], (1,)))
+    far = jnp.stack(held)
+    near = [far, along_z(far, (1, 1)), jnp.concatenate(two_away(far)), along_z(far, (-1, -1))]
+    near = jnp.stack(near)
+    return near, other_core(near)
+
+
+def places(z, core, sign):
+    sense, steps = SENSE[core], STEPS[core]
+    near = [(0, steps), (sign, steps)]
+    near += [(2 * sign * way * sense, steps[part]) for way, part in TWO_AWAY] + [(-sign, steps)]
+    return [(z + d + sign * sense * NEAR * k) % (FAR * NEAR) for d, ks in near for k in ks]
+
+
+def devices(n, sign):
+    cores = [n % 2, 1 - n % 2]
+    return [z * 2 + (c ^ p) for c in cores for z in places(n // 2, c, sign) for p in range(2)]
 
 
 def arrival(n):
-    order = []
-    for x in range(2):
-        for steps in NEAR_STEPS:
-            z, c = divmod(moved(n ^ x, steps, -1), 2)
-            order += [(a * NEAR + z % NEAR) * 2 + c for a in range(FAR)]
-    return order
+    return devices(n, -1)
+
+
+def departure(n):
+    return devices(n, 1)
 
 
 def summed(kept, sent):
     kept = kept + other_core(sent).astype(f32)
     sent = kept.astype(bf16)
-    got = [along_z(sent[s], NEAR_STEPS[s]) for s in (2, 1, 3)]
-    kept = kept[0] + got[0].astype(f32) + got[1].astype(f32) + got[2].astype(f32)
-    half = FAR // 2
-    on, back = kept[half].astype(bf16), kept[half + 1].astype(bf16)
-    for k in range(half - 1, 0, -1):
-        on = (along_z(on, (NEAR, -NEAR)).astype(f32) + kept[k]).astype(bf16)
-        if k > 1:
-            back = (along_z(back, (-NEAR, NEAR)).astype(f32) + kept[FAR + 1 - k]).astype(bf16)
-    return kept[0] + along_z(on, (NEAR, -NEAR)).astype(f32) + along_z(back, (-NEAR, NEAR)).astype(f32)
-
-
-def departure(n):
-    return [
-        moved(moved(n ^ x, steps), (NEAR * k, -NEAR * k))
-        for x in range(2)
-        for steps in NEAR_STEPS
-        for k in range(FAR)
-    ]
+    with_it, against = two_away_terms(sent[2])
+    up, down = along_z(sent[1], (1, 1)), along_z(sent[3], (-1, -1))
+    terms = [kept[0, k] + up[k].astype(f32) + down[k].astype(f32) for k in range(4)]
+    terms[1] += against[0].astype(f32)
+    terms[2] += with_it[0].astype(f32) + against[1].astype(f32)
+    terms[3] += with_it[1].astype(f32)
+    total = passed_on(terms[0].astype(bf16), (1,)).astype(f32)
+    for k in (3, 2, 1):
+        total = passed_on((total + terms[k]).astype(bf16)).astype(f32)
+    total += of_core(terms[0], 0.0)
+    return total + other_core(total)[::-1]
+
+
+def two_away_terms(x):
+    return [along_z(x[2 * i : 2 * i + 2], (-2 * way, 2 * way)) for i, (way, _) in enumerate(TWO_AWAY)]
 
 
 def whole_attention(queries, keys, values, live_lengths, score_scale):
@@ -211,7 +233,8 @@
     order = lax.dynamic_index_in_dim(jnp.asarray(tables), me, keepdims=False)
     live_lengths = lax.dynamic_slice_in_dim(lengths, (me * entries) % ROWS, entries)
     attended = whole_attention(queries, keys, values, live_lengths, queries.shape[2] ** (-0.5))
-    mine, theirs = gathered(attended.reshape(entries, -1))
+    attended = attended.reshape(entries, -1)
+    mine, theirs = gathered(jnp.stack([attended, other_core(attended)]))
 
     width = residual.shape[1]
     half = DEVICES // 2
@@ -249,13 +272,13 @@
         up_weight,
     )
 
-    terms = (NEAR, FAR, SHARE, share_cols)
+    terms = (NEAR, FAR // 2, 2, SHARE, share_cols)
     share = summed(kept.reshape(terms), sent.reshape(terms))
     cols = SHARE * BLK
     weights = 1.0 + jnp.arange(LANES, dtype=f32) / LANES
-    square_sums = jnp.sum(share[:, 2 * cols :], axis=1, keepdims=True) / jnp.sum(weights)
+    square_sums = jnp.sum(share[..., 2 * cols :], axis=-1, keepdims=True) / jnp.sum(weights)
     inverse = 1.0 / (square_sums / D + 1e-05)
-    activated = jnp.maximum(share[:, :cols], 0.0) * share[:, cols : 2 * cols] * inverse
+    activated = jnp.maximum(share[..., :cols], 0.0) * share[..., cols : 2 * cols] * inverse
     mine, theirs = gathered(activated.astype(bf16))
 
     return pl.pallas_call(

time: 207 us -> 179 us (0.86)
  blocking collectives: 80.1 us -> 0 us
  waiting for transfers between devices: 39.5 us -> 88.4 us
  starting transfers between devices: 54.9 us -> 57.5 us
    all_gather x2 -> x0, blocking collectives: 80.1 us -> none  [gathered(): mine = lax.all_gather(x, 'far', axis=0)]
    ppermute x19 -> x29, waiting for transfers between devices: 39.5 us -> 88.4 us  [the longest x24 83.4 us: along_z(): return lax.ppermute(x, AXES, pairs)]
    ppermute x19 -> x29, starting transfers between devices: 54.9 us -> 57.5 us  [the longest x24 34.9 us: along_z(): return lax.ppermute(x, AXES, pairs)]
  transfers between devices with their start and end apart: 19 -> 29, of which waited for: 15 -> 19; matrix products, arithmetic and copies ran while one was open for 2% -> 2% of each run, Pallas kernels for 0% -> 0%
where the time goes in v2:
time: 179 us
  waiting for transfers between devices  88.4 us (49%)
  starting transfers between devices  57.5 us (32%)
  Pallas kernels  18.5 us (10%)
  local copies, waits for them, and re-layouts  5.9 us (3%)
  other arithmetic  4.52 us (3%)
  matrix products  3.59 us (2%)
    ppermute x24, waiting for transfers between devices, along_z(): return lax.ppermute(x, AXES, pairs)  83.4 us
    ppermute x24, starting transfers between devices, along_z(): return lax.ppermute(x, AXES, pairs)  34.9 us
    ppermute x5, starting transfers between devices, other_core(): return lax.ppermute(x, 'core', [(0, 1), (1, 0)])  22.6 us
    pallas_call x1, Pallas kernels, body(): pl.pallas_call(up_kernel, in_specs=[SMEM, SMEM, VMEM, VMEM, VMEM, VMEM, V...  11.8 us
    pallas_call x1, Pallas kernels, body(): pl.pallas_call(down_kernel, in_specs=[SMEM, SMEM, VMEM, VMEM, VMEM, HBM],...  6.69 us
    ppermute x5, waiting for transfers between devices, other_core(): return lax.ppermute(x, 'core', [(0, 1), (1, 0)])  4.99 us
  transfers between devices with their start and end apart: 29, of which 19 were waited for; matrix products, arithmetic and copies ran while one was open for 2% of the time, Pallas kernels for 0%

profile of v2, /device:TPU:37, one launch (start us, length us, event | category | flops | bytes accessed | tf_op | source)
XLA Modules:
  0.0 178.8 jit_solution(3341066585490197957)
XLA Ops:
  0.0 0.9 dynamic_slice.8
  1.0 0.6 copy-done
  1.6 1.5 fusion.29
  3.2 2.1 %convolution_convert_fusion = bf16[8,8,128]{2,1,0:T(8,128)(2,1)S(1)} fusion(bf16[8,1024,128]{2,1,0:T(8,128)(2,1)} %param.14, f32[8,8,1024]{2,1,0:T(8,128)S(1)} %get-tuple-element.26, f32[8,8]{1,0:T(8,128)S(1)} %get-tuple-element.25), kind=kOutput, calls=%fused_computation.7 | convolution fusion | flops 16916480 | bytes 2375936 | tf_op jit(solution)/shard_map/egt,etc->egc/dot_general | solution.py:110
  5.2 20.5 %collective-permute-start = (bf16[8,1024]{1,0:T(8,128)(2,1)S(1)}, bf16[8,1024]{1,0:T(8,128)(2,1)S(1)}, u32[]{:S(2)}, u32[]{:S(2)}) collective-permute-start(bf16[8,1024]{1,0:T(8,128)(2,1)S(1)} %bitcast.186), channel_id=1, source_target_pairs={{0,1},{1,0},{2,3},{3,2},{4,5},{5,4},{6,7},{7,6},{8,9},{9,8},{10,11... | collective-permute-start | bytes 49160 | tf_op jit(solution)/shard_map/ppermute | solution.py:43
  25.8 0.8 collective-permute-done
  26.6 6.7 %collective-permute-done.1 = bf16[2,8,1024]{2,1,0:T(8,128)(2,1)S(1)} collective-permute-done((bf16[2,8,1024]{2,1,0:T(8,128)(2,1)S(1)}, bf16[2,8,1024]{2,1,0:T(8,128)(2,1)S(1)}, u32[]{:S(2)}, u32[]{:S(2)}) %collective-permute-start.1) | collective-permute-done | bytes 32800 | tf_op jit(solution)/shard_map/ppermute | solution.py:31
  33.3 6.8 %collective-permute-done.2 = bf16[2,8,1024]{2,1,0:T(8,128)(2,1)S(1)} collective-permute-done((bf16[2,8,1024]{2,1,0:T(8,128)(2,1)S(1)}, bf16[2,8,1024]{2,1,0:T(8,128)(2,1)S(1)}, u32[]{:S(2)}, u32[]{:S(2)}) %collective-permute-start.2) | collective-permute-done | bytes 32800 | tf_op jit(solution)/shard_map/ppermute | solution.py:31
  40.1 6.8 %collective-permute-done.3 = bf16[2,8,1024]{2,1,0:T(8,128)(2,1)S(1)} collective-permute-done((bf16[2,8,1024]{2,1,0:T(8,128)(2,1)S(1)}, bf16[2,8,1024]{2,1,0:T(8,128)(2,1)S(1)}, u32[]{:S(2)}, u32[]{:S(2)}) %collective-permute-start.3) | collective-permute-done | bytes 32800 | tf_op jit(solution)/shard_map/ppermute | solution.py:31
  46.8 1.9 %collective-permute-start.4 = (bf16[2,8,1024]{2,1,0:T(8,128)(2,1)S(1)}, bf16[2,8,1024]{2,1,0:T(8,128)(2,1)S(1)}, u32[]{:S(2)}, u32[]{:S(2)}) collective-permute-start(bf16[2,8,1024]{2,1,0:T(8,128)(2,1)S(1)} %collective-permute-done.3), channel_id=1, source_target_pairs={{1,9},{3,11},{5,13},{7,15},{9,17},{11,19},{13,21},{15,23},{17,25},... | collective-permute-start | bytes 98312 | tf_op jit(solution)/shard_map/ppermute | solution.py:31
  48.8 2.7 %collective-permute-start.6 = (bf16[2,2,8,1024]{3,2,1,0:T(8,128)(2,1)S(1)}, bf16[2,2,8,1024]{3,2,1,0:T(8,128)(2,1)S(1)}, u32[]{:S(2)}, u32[]{:S(2)}) collective-permute-start(bf16[2,2,8,1024]{3,2,1,0:T(8,128)(2,1)S(1)} %get-tuple-element.23), channel_id=1, source_target_pairs={{0,60},{1,5},{2,62},{3,7},{4,0},{5,9},{6,2},{7,11},{8,4},{9,13},{1... | collective-permute-start | bytes 196616 | tf_op jit(solution)/shard_map/ppermute | solution.py:31
  51.5 3.3 %collective-permute-start.7 = (bf16[2,2,8,1024]{3,2,1,0:T(8,128)(2,1)S(1)}, bf16[2,2,8,1024]{3,2,1,0:T(8,128)(2,1)S(1)}, u32[]{:S(2)}, u32[]{:S(2)}) collective-permute-start(bf16[2,2,8,1024]{3,2,1,0:T(8,128)(2,1)S(1)} %get-tuple-element.24), channel_id=1, source_target_pairs={{0,4},{1,61},{2,6},{3,63},{4,8},{5,1},{6,10},{7,3},{8,12},{9,5},{1... | collective-permute-start | bytes 196616 | tf_op jit(solution)/shard_map/ppermute | solution.py:31
  54.8 0.6 collective-permute-done.4
  55.5 1.6 collective-permute-start.5
  57.2 5.2 %collective-permute-start.8 = (bf16[4,2,8,1024]{3,2,1,0:T(8,128)(2,1)S(1)}, bf16[4,2,8,1024]{3,2,1,0:T(8,128)(2,1)S(1)}, u32[]{:S(2)}, u32[]{:S(2)}) collective-permute-start(bf16[4,2,8,1024]{3,2,1,0:T(8,128)(2,1)S(1)} %get-tuple-element.20), channel_id=1, source_target_pairs={{0,62},{1,63},{2,0},{3,1},{4,2},{5,3},{6,4},{7,5},{8,6},{9,7},{10,... | collective-permute-start | bytes 393224 | tf_op jit(solution)/shard_map/ppermute | solution.py:31
  62.4 2.2 %collective-permute-done.5 = bf16[4,2,8,1024]{3,2,1,0:T(8,128)(2,1)S(1)} collective-permute-done((bf16[4,2,8,1024]{3,2,1,0:T(8,128)(2,1)S(1)}, bf16[4,2,8,1024]{3,2,1,0:T(8,128)(2,1)S(1)}, u32[]{:S(2)}, u32[]{:S(2)}) %collective-permute-start.5) | collective-permute-done | bytes 131104 | tf_op jit(solution)/shard_map/ppermute | solution.py:31
  64.8 0.7 copy.13.residual
  65.5 1.3 dynamic-slice_bitcast_fusion.order
  67.3 0.8 copy-done.3
  68.1 11.8 %up_kernel.1 = (f32[128,64]{1,0:T(8,128)}, f32[32,8,2176]{2,1,0:T(8,128)}, bf16[32,8,2176]{2,1,0:T(8,128)(2,1)}) custom-call(s32[2,64]{1,0:T(2,128)} %dynamic-slice_bitcast_fusion.order, s32[16,32]{1,0:T(8,128)} %active.3, bf16[32,8,1024]{2,1,0:T(8,128)(2,1)} %bitcast.160, bf16[32,8,1024]{2,1,0:T(8,128)(2,1)} %bitcast.164, bf16[128,64]{1,0:T(8,128)(2,1)} %copy.13.residual, ...), custom_call_target="tpu_custom_call" | custom-call | tf_op jit(solution)/shard_map/up_kernel/pallas_call | solution.py:244
  79.9 0.8 collective-permute-start.10
  80.7 2.6 %collective-permute-done.10 = bf16[4,4,2,8,2176]{4,3,2,1,0:T(8,128)(2,1)S(1)} collective-permute-done((bf16[4,4,2,8,2176]{4,3,2,1,0:T(8,128)(2,1)}, bf16[4,4,2,8,2176]{4,3,2,1,0:T(8,128)(2,1)S(1)}, u32[]{:S(2)}, u32[]{:S(2)}) %collective-permute-start.10) | collective-permute-done | bytes 1114144 | tf_op jit(solution)/shard_map/ppermute | solution.py:43
  83.3 1.9 %fusion.28 = (bf16[4,4,2,8,2176]{4,3,2,1,0:T(8,128)(2,1)S(1)}, f32[4,4,2,8,2176]{4,3,2,1,0:T(8,128)S(1)}) fusion(f32[4,4,2,8,2176]{4,3,2,1,0:T(8,128)} %bitcast.159, bf16[4,4,2,8,2176]{4,3,2,1,0:T(8,128)(2,1)S(1)} %collective-permute-done.10), kind=kLoop, calls=%fused_computation.74 | loop fusion | flops 1671168 | bytes 6684672 | tf_op jit(solution)/shard_map/convert_element_type | solution.py:83
  85.4 2.9 %collective-permute-start.12 = (bf16[4,2,8,2176]{3,2,1,0:T(8,128)(2,1)S(1)}, bf16[4,2,8,2176]{3,2,1,0:T(8,128)(2,1)S(1)}, u32[]{:S(2)}, u32[]{:S(2)}) collective-permute-start(bf16[4,2,8,2176]{3,2,1,0:T(8,128)(2,1)S(1)} %get-tuple-element.16), channel_id=1, source_target_pairs={{0,62},{1,63},{2,0},{3,1},{4,2},{5,3},{6,4},{7,5},{8,6},{9,7},{10,... | collective-permute-start | bytes 835592 | tf_op jit(solution)/shard_map/ppermute | solution.py:31
  88.5 6.2 %collective-permute-done.11 = bf16[4,2,8,2176]{3,2,1,0:T(8,128)(2,1)S(1)} collective-permute-done((bf16[4,2,8,2176]{3,2,1,0:T(8,128)(2,1)S(1)}, bf16[4,2,8,2176]{3,2,1,0:T(8,128)(2,1)S(1)}, u32[]{:S(2)}, u32[]{:S(2)}) %collective-permute-start.11) | collective-permute-done | bytes 278560 | tf_op jit(solution)/shard_map/ppermute | solution.py:31
  94.7 2.7 %collective-permute-start.13 = (bf16[2,8,2176]{2,1,0:T(8,128)(2,1)S(1)}, bf16[2,8,2176]{2,1,0:T(8,128)(2,1)S(1)}, u32[]{:S(2)}, u32[]{:S(2)}) collective-permute-start(bf16[2,8,2176]{2,1,0:T(8,128)(2,1)S(1)} %fusion.25), channel_id=1, source_target_pairs={{1,9},{3,11},{5,13},{7,15},{9,17},{11,19},{13,21},{15,23},{17,25},... | collective-permute-start | bytes 208904 | tf_op jit(solution)/shard_map/ppermute | solution.py:31
  97.4 2.3 %collective-permute-start.16 = (bf16[2,2,8,2176]{3,2,1,0:T(8,128)(2,1)S(1)}, bf16[2,2,8,2176]{3,2,1,0:T(8,128)(2,1)S(1)}, u32[]{:S(2)}, u32[]{:S(2)}) collective-permute-start(bf16[2,2,8,2176]{3,2,1,0:T(8,128)(2,1)S(1)} %get-tuple-element.13), channel_id=1, source_target_pairs={{0,4},{1,61},{2,6},{3,63},{4,8},{5,1},{6,10},{7,3},{8,12},{9,5},{1... | collective-permute-start | bytes 417800 | tf_op jit(solution)/shard_map/ppermute | solution.py:31
  99.7 4.1 %collective-permute-done.13 = bf16[2,8,2176]{2,1,0:T(8,128)(2,1)S(1)} collective-permute-done((bf16[2,8,2176]{2,1,0:T(8,128)(2,1)S(1)}, bf16[2,8,2176]{2,1,0:T(8,128)(2,1)S(1)}, u32[]{:S(2)}, u32[]{:S(2)}) %collective-permute-start.13) | collective-permute-done | bytes 69664 | tf_op jit(solution)/shard_map/ppermute | solution.py:31
  103.9 1.2 collective-permute-start.15
  105.1 8.2 %collective-permute-done.15 = bf16[2,8,2176]{2,1,0:T(8,128)(2,1)S(1)} collective-permute-done((bf16[2,8,2176]{2,1,0:T(8,128)(2,1)S(1)}, bf16[2,8,2176]{2,1,0:T(8,128)(2,1)S(1)}, u32[]{:S(2)}, u32[]{:S(2)}) %collective-permute-start.15) | collective-permute-done | bytes 69664 | tf_op jit(solution)/shard_map/ppermute | solution.py:31
  113.5 7.6 %collective-permute-done.17 = bf16[2,8,2176]{2,1,0:T(8,128)(2,1)S(1)} collective-permute-done((bf16[2,8,2176]{2,1,0:T(8,128)(2,1)S(1)}, bf16[2,8,2176]{2,1,0:T(8,128)(2,1)S(1)}, u32[]{:S(2)}, u32[]{:S(2)}) %collective-permute-start.17) | collective-permute-done | bytes 69664 | tf_op jit(solution)/shard_map/ppermute | solution.py:31
  121.3 7.3 %collective-permute-done.18 = bf16[2,8,2176]{2,1,0:T(8,128)(2,1)S(1)} collective-permute-done((bf16[2,8,2176]{2,1,0:T(8,128)(2,1)S(1)}, bf16[2,8,2176]{2,1,0:T(8,128)(2,1)S(1)}, u32[]{:S(2)}, u32[]{:S(2)}) %collective-permute-start.18) | collective-permute-done | bytes 69664 | tf_op jit(solution)/shard_map/ppermute | solution.py:31
  129.5 0.7 collective-permute-done.19
  130.3 0.7 add_divide_fusion
  131.1 6.6 %collective-permute-done.20 = bf16[2,8,1024]{2,1,0:T(8,128)(2,1)S(1)} collective-permute-done((bf16[2,8,1024]{2,1,0:T(8,128)(2,1)S(1)}, bf16[2,8,1024]{2,1,0:T(8,128)(2,1)S(1)}, u32[]{:S(2)}, u32[]{:S(2)}) %collective-permute-start.20) | collective-permute-done | bytes 32800 | tf_op jit(solution)/shard_map/ppermute | solution.py:31
  137.8 6.7 %collective-permute-done.21 = bf16[2,8,1024]{2,1,0:T(8,128)(2,1)S(1)} collective-permute-done((bf16[2,8,1024]{2,1,0:T(8,128)(2,1)S(1)}, bf16[2,8,1024]{2,1,0:T(8,128)(2,1)S(1)}, u32[]{:S(2)}, u32[]{:S(2)}) %collective-permute-start.21) | collective-permute-done | bytes 32800 | tf_op jit(solution)/shard_map/ppermute | solution.py:31
  144.5 6.7 %collective-permute-done.22 = bf16[2,8,1024]{2,1,0:T(8,128)(2,1)S(1)} collective-permute-done((bf16[2,8,1024]{2,1,0:T(8,128)(2,1)S(1)}, bf16[2,8,1024]{2,1,0:T(8,128)(2,1)S(1)}, u32[]{:S(2)}, u32[]{:S(2)}) %collective-permute-start.22) | collective-permute-done | bytes 32800 | tf_op jit(solution)/shard_map/ppermute | solution.py:31
  151.2 1.9 %collective-permute-start.23 = (bf16[2,8,1024]{2,1,0:T(8,128)(2,1)S(1)}, bf16[2,8,1024]{2,1,0:T(8,128)(2,1)S(1)}, u32[]{:S(2)}, u32[]{:S(2)}) collective-permute-start(bf16[2,8,1024]{2,1,0:T(8,128)(2,1)S(1)} %collective-permute-done.22), channel_id=1, source_target_pairs={{1,9},{3,11},{5,13},{7,15},{9,17},{11,19},{13,21},{15,23},{17,25},... | collective-permute-start | bytes 98312 | tf_op jit(solution)/shard_map/ppermute | solution.py:31
  153.1 1.6 collective-permute-start.25
  154.7 2.1 %collective-permute-start.26 = (bf16[2,2,8,1024]{3,2,1,0:T(8,128)(2,1)S(1)}, bf16[2,2,8,1024]{3,2,1,0:T(8,128)(2,1)S(1)}, u32[]{:S(2)}, u32[]{:S(2)}) collective-permute-start(bf16[2,2,8,1024]{3,2,1,0:T(8,128)(2,1)S(1)} %get-tuple-element.22), channel_id=1, source_target_pairs={{0,4},{1,61},{2,6},{3,63},{4,8},{5,1},{6,10},{7,3},{8,12},{9,5},{1... | collective-permute-start | bytes 196616 | tf_op jit(solution)/shard_map/ppermute | solution.py:31
  156.8 2.9 %collective-permute-done.23 = bf16[2,8,1024]{2,1,0:T(8,128)(2,1)S(1)} collective-permute-done((bf16[2,8,1024]{2,1,0:T(8,128)(2,1)S(1)}, bf16[2,8,1024]{2,1,0:T(8,128)(2,1)S(1)}, u32[]{:S(2)}, u32[]{:S(2)}) %collective-permute-start.23) | collective-permute-done | bytes 32800 | tf_op jit(solution)/shard_map/ppermute | solution.py:31
  160.0 4.6 %collective-permute-start.27 = (bf16[4,2,8,1024]{3,2,1,0:T(8,128)(2,1)S(1)}, bf16[4,2,8,1024]{3,2,1,0:T(8,128)(2,1)S(1)}, u32[]{:S(2)}, u32[]{:S(2)}) collective-permute-start(bf16[4,2,8,1024]{3,2,1,0:T(8,128)(2,1)S(1)} %get-tuple-element.18), channel_id=1, source_target_pairs={{0,62},{1,63},{2,0},{3,1},{4,2},{5,3},{6,4},{7,5},{8,6},{9,7},{10,... | collective-permute-start | bytes 393224 | tf_op jit(solution)/shard_map/ppermute | solution.py:31
  164.7 3.9 %collective-permute-done.24 = bf16[4,2,8,1024]{3,2,1,0:T(8,128)(2,1)S(1)} collective-permute-done((bf16[4,2,8,1024]{3,2,1,0:T(8,128)(2,1)S(1)}, bf16[4,2,8,1024]{3,2,1,0:T(8,128)(2,1)S(1)}, u32[]{:S(2)}, u32[]{:S(2)}) %collective-permute-start.24) | collective-permute-done | bytes 131104 | tf_op jit(solution)/shard_map/ppermute | solution.py:31
  168.7 1.0 collective-permute-start.28
  169.6 0.7 copy.14
  170.3 0.8 collective-permute-done.28
  171.2 0.8 copy-done.4
  171.9 6.7 %down_kernel.1 = bf16[64,128]{1,0:T(8,128)(2,1)} custom-call(s32[2,64]{1,0:T(2,128)} %dynamic-slice_bitcast_fusion.order, s32[16,32]{1,0:T(8,128)} %active.3, bf16[32,8,1024]{2,1,0:T(8,128)(2,1)} %bitcast.161, bf16[32,8,1024]{2,1,0:T(8,128)(2,1)} %bitcast.165, f32[64,128]{1,0:T(8,128)} %bitcast.167, bf16[64,14336]{1,0:T(8,128)(2,1)} %bitcast.162), custom_call_target="tpu_custom_call" | custom-call | tf_op jit(solution)/shard_map/down_kernel/pallas_call | solution.py:284
  (62 shorter events, 3.1 us)
Async XLA Ops:
  0.0 1.6 copy-start
  3.1 61.6 %copy-start.6 = (bf16[128,64]{0,1:T(8,128)(2,1)S(1)}, bf16[128,64]{0,1:T(8,128)(2,1)}, u32[]{:S(2)}) copy-start(bf16[128,64]{0,1:T(8,128)(2,1)} %param.17) | copy-start | bytes 49156
  3.1 63.6 %copy-start.7 = (bf16[64]{0:T(256)(128)(2,1)S(1)}, bf16[64]{0:T(256)(128)(2,1)}, u32[]{:S(2)}) copy-start(bf16[64]{0:T(256)(128)(2,1)} %param.19) | copy-start | bytes 388
  5.2 21.4 %collective-permute-start = (bf16[8,1024]{1,0:T(8,128)(2,1)S(1)}, bf16[8,1024]{1,0:T(8,128)(2,1)S(1)}, u32[]{:S(2)}, u32[]{:S(2)}) collective-permute-start(bf16[8,1024]{1,0:T(8,128)(2,1)S(1)} %bitcast.186), channel_id=1, source_target_pairs={{0,1},{1,0},{2,3},{3,2},{4,5},{5,4},{6,7},{7,6},{8,9},{9,8},{10,11... | collective-permute-start | bytes 49160 | tf_op jit(solution)/shard_map/ppermute | solution.py:43
  26.6 6.7 %collective-permute-start.1 = (bf16[2,8,1024]{2,1,0:T(8,128)(2,1)S(1)}, bf16[2,8,1024]{2,1,0:T(8,128)(2,1)S(1)}, u32[]{:S(2)}, u32[]{:S(2)}) collective-permute-start(bf16[2,8,1024]{2,1,0:T(8,128)(2,1)S(1)} %pad_maximum_fusion.8), channel_id=1, source_target_pairs={{0,56},{1,9},{2,58},{3,11},{4,60},{5,13},{6,62},{7,15},{8,0},{9,17... | collective-permute-start | bytes 98312 | tf_op jit(solution)/shard_map/ppermute | solution.py:31
  33.3 6.8 %collective-permute-start.2 = (bf16[2,8,1024]{2,1,0:T(8,128)(2,1)S(1)}, bf16[2,8,1024]{2,1,0:T(8,128)(2,1)S(1)}, u32[]{:S(2)}, u32[]{:S(2)}) collective-permute-start(bf16[2,8,1024]{2,1,0:T(8,128)(2,1)S(1)} %collective-permute-done.1), channel_id=1, source_target_pairs={{0,56},{1,9},{2,58},{3,11},{4,60},{5,13},{6,62},{7,15},{8,0},{9,17... | collective-permute-start | bytes 98312 | tf_op jit(solution)/shard_map/ppermute | solution.py:31
  40.1 6.8 %collective-permute-start.3 = (bf16[2,8,1024]{2,1,0:T(8,128)(2,1)S(1)}, bf16[2,8,1024]{2,1,0:T(8,128)(2,1)S(1)}, u32[]{:S(2)}, u32[]{:S(2)}) collective-permute-start(bf16[2,8,1024]{2,1,0:T(8,128)(2,1)S(1)} %collective-permute-done.2), channel_id=1, source_target_pairs={{0,56},{1,9},{2,58},{3,11},{4,60},{5,13},{6,62},{7,15},{8,0},{9,17... | collective-permute-start | bytes 98312 | tf_op jit(solution)/shard_map/ppermute | solution.py:31
  46.8 8.6 %collective-permute-start.4 = (bf16[2,8,1024]{2,1,0:T(8,128)(2,1)S(1)}, bf16[2,8,1024]{2,1,0:T(8,128)(2,1)S(1)}, u32[]{:S(2)}, u32[]{:S(2)}) collective-permute-start(bf16[2,8,1024]{2,1,0:T(8,128)(2,1)S(1)} %collective-permute-done.3), channel_id=1, source_target_pairs={{1,9},{3,11},{5,13},{7,15},{9,17},{11,19},{13,21},{15,23},{17,25},... | collective-permute-start | bytes 98312 | tf_op jit(solution)/shard_map/ppermute | solution.py:31
  48.8 13.5 %collective-permute-start.6 = (bf16[2,2,8,1024]{3,2,1,0:T(8,128)(2,1)S(1)}, bf16[2,2,8,1024]{3,2,1,0:T(8,128)(2,1)S(1)}, u32[]{:S(2)}, u32[]{:S(2)}) collective-permute-start(bf16[2,2,8,1024]{3,2,1,0:T(8,128)(2,1)S(1)} %get-tuple-element.23), channel_id=1, source_target_pairs={{0,60},{1,5},{2,62},{3,7},{4,0},{5,9},{6,2},{7,11},{8,4},{9,13},{1... | collective-permute-start | bytes 196616 | tf_op jit(solution)/shard_map/ppermute | solution.py:31
  51.5 10.8 %collective-permute-start.7 = (bf16[2,2,8,1024]{3,2,1,0:T(8,128)(2,1)S(1)}, bf16[2,2,8,1024]{3,2,1,0:T(8,128)(2,1)S(1)}, u32[]{:S(2)}, u32[]{:S(2)}) collective-permute-start(bf16[2,2,8,1024]{3,2,1,0:T(8,128)(2,1)S(1)} %get-tuple-element.24), channel_id=1, source_target_pairs={{0,4},{1,61},{2,6},{3,63},{4,8},{5,1},{6,10},{7,3},{8,12},{9,5},{1... | collective-permute-start | bytes 196616 | tf_op jit(solution)/shard_map/ppermute | solution.py:31
  55.5 9.1 %collective-permute-start.5 = (bf16[4,2,8,1024]{3,2,1,0:T(8,128)(2,1)S(1)}, bf16[4,2,8,1024]{3,2,1,0:T(8,128)(2,1)S(1)}, u32[]{:S(2)}, u32[]{:S(2)}) collective-permute-start(bf16[4,2,8,1024]{3,2,1,0:T(8,128)(2,1)S(1)} %get-tuple-element.20), channel_id=1, source_target_pairs={{0,2},{1,3},{2,4},{3,5},{4,6},{5,7},{6,8},{7,9},{8,10},{9,11},{10,... | collective-permute-start | bytes 393224 | tf_op jit(solution)/shard_map/ppermute | solution.py:31
  57.2 7.4 %collective-permute-start.8 = (bf16[4,2,8,1024]{3,2,1,0:T(8,128)(2,1)S(1)}, bf16[4,2,8,1024]{3,2,1,0:T(8,128)(2,1)S(1)}, u32[]{:S(2)}, u32[]{:S(2)}) collective-permute-start(bf16[4,2,8,1024]{3,2,1,0:T(8,128)(2,1)S(1)} %get-tuple-element.20), channel_id=1, source_target_pairs={{0,62},{1,63},{2,0},{3,1},{4,2},{5,3},{6,4},{7,5},{8,6},{9,7},{10,... | collective-permute-start | bytes 393224 | tf_op jit(solution)/shard_map/ppermute | solution.py:31
  64.6 2.7 %copy-start.1 = (bf16[4,4,2,8,1024]{4,3,2,1,0:T(8,128)(2,1)}, bf16[4,4,2,8,1024]{4,3,2,1,0:T(8,128)(2,1)S(1)}, u32[]{:S(2)}) copy-start(bf16[4,4,2,8,1024]{4,3,2,1,0:T(8,128)(2,1)S(1)} %pad_maximum_fusion) | copy-start | bytes 1572868
  64.6 2.7 %collective-permute-start.9 = (bf16[4,4,2,8,1024]{4,3,2,1,0:T(8,128)(2,1)S(1)}, bf16[4,4,2,8,1024]{4,3,2,1,0:T(8,128)(2,1)S(1)}, u32[]{:S(2)}, u32[]{:S(2)}) collective-permute-start(bf16[4,4,2,8,1024]{4,3,2,1,0:T(8,128)(2,1)S(1)} %pad_maximum_fusion), channel_id=1, source_target_pairs={{0,1},{1,0},{2,3},{3,2},{4,5},{5,4},{6,7},{7,6},{8,9},{9,8},{10,11... | collective-permute-start | bytes 1572872 | tf_op jit(solution)/shard_map/ppermute | solution.py:43
  67.3 0.8 copy-start.3
  79.9 3.4 %collective-permute-start.10 = (bf16[4,4,2,8,2176]{4,3,2,1,0:T(8,128)(2,1)}, bf16[4,4,2,8,2176]{4,3,2,1,0:T(8,128)(2,1)S(1)}, u32[]{:S(2)}, u32[]{:S(2)}) collective-permute-start(bf16[4,4,2,8,2176]{4,3,2,1,0:T(8,128)(2,1)} %bitcast.187), channel_id=1, source_target_pairs={{0,1},{1,0},{2,3},{3,2},{4,5},{5,4},{6,7},{7,6},{8,9},{9,8},{10,11... | collective-permute-start | bytes 3342344 | tf_op jit(solution)/shard_map/ppermute | solution.py:43
  85.3 9.4 %collective-permute-start.11 = (bf16[4,2,8,2176]{3,2,1,0:T(8,128)(2,1)S(1)}, bf16[4,2,8,2176]{3,2,1,0:T(8,128)(2,1)S(1)}, u32[]{:S(2)}, u32[]{:S(2)}) collective-permute-start(bf16[4,2,8,2176]{3,2,1,0:T(8,128)(2,1)S(1)} %get-tuple-element.15), channel_id=1, source_target_pairs={{0,2},{1,3},{2,4},{3,5},{4,6},{5,7},{6,8},{7,9},{8,10},{9,11},{10,... | collective-permute-start | bytes 835592 | tf_op jit(solution)/shard_map/ppermute | solution.py:31
  85.4 9.3 %collective-permute-start.12 = (bf16[4,2,8,2176]{3,2,1,0:T(8,128)(2,1)S(1)}, bf16[4,2,8,2176]{3,2,1,0:T(8,128)(2,1)S(1)}, u32[]{:S(2)}, u32[]{:S(2)}) collective-permute-start(bf16[4,2,8,2176]{3,2,1,0:T(8,128)(2,1)S(1)} %get-tuple-element.16), channel_id=1, source_target_pairs={{0,62},{1,63},{2,0},{3,1},{4,2},{5,3},{6,4},{7,5},{8,6},{9,7},{10,... | collective-permute-start | bytes 835592 | tf_op jit(solution)/shard_map/ppermute | solution.py:31
  88.3 11.4 %collective-permute-start.14 = (bf16[2,2,8,2176]{3,2,1,0:T(8,128)(2,1)S(1)}, bf16[2,2,8,2176]{3,2,1,0:T(8,128)(2,1)S(1)}, u32[]{:S(2)}, u32[]{:S(2)}) collective-permute-start(bf16[2,2,8,2176]{3,2,1,0:T(8,128)(2,1)S(1)} %get-tuple-element.14), channel_id=1, source_target_pairs={{0,60},{1,5},{2,62},{3,7},{4,0},{5,9},{6,2},{7,11},{8,4},{9,13},{1... | collective-permute-start | bytes 417800 | tf_op jit(solution)/shard_map/ppermute | solution.py:31
  94.7 9.1 %collective-permute-start.13 = (bf16[2,8,2176]{2,1,0:T(8,128)(2,1)S(1)}, bf16[2,8,2176]{2,1,0:T(8,128)(2,1)S(1)}, u32[]{:S(2)}, u32[]{:S(2)}) collective-permute-start(bf16[2,8,2176]{2,1,0:T(8,128)(2,1)S(1)} %fusion.25), channel_id=1, source_target_pairs={{1,9},{3,11},{5,13},{7,15},{9,17},{11,19},{13,21},{15,23},{17,25},... | collective-permute-start | bytes 208904 | tf_op jit(solution)/shard_map/ppermute | solution.py:31
  97.4 7.7 %collective-permute-start.16 = (bf16[2,2,8,2176]{3,2,1,0:T(8,128)(2,1)S(1)}, bf16[2,2,8,2176]{3,2,1,0:T(8,128)(2,1)S(1)}, u32[]{:S(2)}, u32[]{:S(2)}) collective-permute-start(bf16[2,2,8,2176]{3,2,1,0:T(8,128)(2,1)S(1)} %get-tuple-element.13), channel_id=1, source_target_pairs={{0,4},{1,61},{2,6},{3,63},{4,8},{5,1},{6,10},{7,3},{8,12},{9,5},{1... | collective-permute-start | bytes 417800 | tf_op jit(solution)/shard_map/ppermute | solution.py:31
  103.9 65.7 %copy-start.5 = (f32[128,64]{1,0:T(8,128)S(1)}, f32[128,64]{1,0:T(8,128)}, u32[]{:S(2)}) copy-start(f32[128,64]{1,0:T(8,128)} %get-tuple-element.10) | copy-start | bytes 98308
  103.9 9.4 %collective-permute-start.15 = (bf16[2,8,2176]{2,1,0:T(8,128)(2,1)S(1)}, bf16[2,8,2176]{2,1,0:T(8,128)(2,1)S(1)}, u32[]{:S(2)}, u32[]{:S(2)}) collective-permute-start(bf16[2,8,2176]{2,1,0:T(8,128)(2,1)S(1)} %fusion.19), channel_id=1, source_target_pairs={{0,56},{1,9},{2,58},{3,11},{4,60},{5,13},{6,62},{7,15},{8,0},{9,17... | collective-permute-start | bytes 208904 | tf_op jit(solution)/shard_map/ppermute | solution.py:31
  113.4 7.8 %collective-permute-start.17 = (bf16[2,8,2176]{2,1,0:T(8,128)(2,1)S(1)}, bf16[2,8,2176]{2,1,0:T(8,128)(2,1)S(1)}, u32[]{:S(2)}, u32[]{:S(2)}) collective-permute-start(bf16[2,8,2176]{2,1,0:T(8,128)(2,1)S(1)} %fusion.14), channel_id=1, source_target_pairs={{0,56},{1,9},{2,58},{3,11},{4,60},{5,13},{6,62},{7,15},{8,0},{9,17... | collective-permute-start | bytes 208904 | tf_op jit(solution)/shard_map/ppermute | solution.py:31
  121.2 7.5 %collective-permute-start.18 = (bf16[2,8,2176]{2,1,0:T(8,128)(2,1)S(1)}, bf16[2,8,2176]{2,1,0:T(8,128)(2,1)S(1)}, u32[]{:S(2)}, u32[]{:S(2)}) collective-permute-start(bf16[2,8,2176]{2,1,0:T(8,128)(2,1)S(1)} %fusion.9), channel_id=1, source_target_pairs={{0,56},{1,9},{2,58},{3,11},{4,60},{5,13},{6,62},{7,15},{8,0},{9,17... | collective-permute-start | bytes 208904 | tf_op jit(solution)/shard_map/ppermute | solution.py:31
  128.7 1.5 collective-permute-start.19
  131.0 6.7 %collective-permute-start.20 = (bf16[2,8,1024]{2,1,0:T(8,128)(2,1)S(1)}, bf16[2,8,1024]{2,1,0:T(8,128)(2,1)S(1)}, u32[]{:S(2)}, u32[]{:S(2)}) collective-permute-start(bf16[2,8,1024]{2,1,0:T(8,128)(2,1)S(1)} %fusion.24), channel_id=1, source_target_pairs={{0,56},{1,9},{2,58},{3,11},{4,60},{5,13},{6,62},{7,15},{8,0},{9,17... | collective-permute-start | bytes 98312 | tf_op jit(solution)/shard_map/ppermute | solution.py:31
  137.8 6.7 %collective-permute-start.21 = (bf16[2,8,1024]{2,1,0:T(8,128)(2,1)S(1)}, bf16[2,8,1024]{2,1,0:T(8,128)(2,1)S(1)}, u32[]{:S(2)}, u32[]{:S(2)}) collective-permute-start(bf16[2,8,1024]{2,1,0:T(8,128)(2,1)S(1)} %collective-permute-done.20), channel_id=1, source_target_pairs={{0,56},{1,9},{2,58},{3,11},{4,60},{5,13},{6,62},{7,15},{8,0},{9,17... | collective-permute-start | bytes 98312 | tf_op jit(solution)/shard_map/ppermute | solution.py:31
  144.4 6.7 %collective-permute-start.22 = (bf16[2,8,1024]{2,1,0:T(8,128)(2,1)S(1)}, bf16[2,8,1024]{2,1,0:T(8,128)(2,1)S(1)}, u32[]{:S(2)}, u32[]{:S(2)}) collective-permute-start(bf16[2,8,1024]{2,1,0:T(8,128)(2,1)S(1)} %collective-permute-done.21), channel_id=1, source_target_pairs={{0,56},{1,9},{2,58},{3,11},{4,60},{5,13},{6,62},{7,15},{8,0},{9,17... | collective-permute-start | bytes 98312 | tf_op jit(solution)/shard_map/ppermute | solution.py:31
  151.2 8.6 %collective-permute-start.23 = (bf16[2,8,1024]{2,1,0:T(8,128)(2,1)S(1)}, bf16[2,8,1024]{2,1,0:T(8,128)(2,1)S(1)}, u32[]{:S(2)}, u32[]{:S(2)}) collective-permute-start(bf16[2,8,1024]{2,1,0:T(8,128)(2,1)S(1)} %collective-permute-done.22), channel_id=1, source_target_pairs={{1,9},{3,11},{5,13},{7,15},{9,17},{11,19},{13,21},{15,23},{17,25},... | collective-permute-start | bytes 98312 | tf_op jit(solution)/shard_map/ppermute | solution.py:31
  153.1 11.5 %collective-permute-start.25 = (bf16[2,2,8,1024]{3,2,1,0:T(8,128)(2,1)S(1)}, bf16[2,2,8,1024]{3,2,1,0:T(8,128)(2,1)S(1)}, u32[]{:S(2)}, u32[]{:S(2)}) collective-permute-start(bf16[2,2,8,1024]{3,2,1,0:T(8,128)(2,1)S(1)} %get-tuple-element.21), channel_id=1, source_target_pairs={{0,60},{1,5},{2,62},{3,7},{4,0},{5,9},{6,2},{7,11},{8,4},{9,13},{1... | collective-permute-start | bytes 196616 | tf_op jit(solution)/shard_map/ppermute | solution.py:31
  154.7 9.9 %collective-permute-start.26 = (bf16[2,2,8,1024]{3,2,1,0:T(8,128)(2,1)S(1)}, bf16[2,2,8,1024]{3,2,1,0:T(8,128)(2,1)S(1)}, u32[]{:S(2)}, u32[]{:S(2)}) collective-permute-start(bf16[2,2,8,1024]{3,2,1,0:T(8,128)(2,1)S(1)} %get-tuple-element.22), channel_id=1, source_target_pairs={{0,4},{1,61},{2,6},{3,63},{4,8},{5,1},{6,10},{7,3},{8,12},{9,5},{1... | collective-permute-start | bytes 196616 | tf_op jit(solution)/shard_map/ppermute | solution.py:31
  159.9 8.7 %collective-permute-start.24 = (bf16[4,2,8,1024]{3,2,1,0:T(8,128)(2,1)S(1)}, bf16[4,2,8,1024]{3,2,1,0:T(8,128)(2,1)S(1)}, u32[]{:S(2)}, u32[]{:S(2)}) collective-permute-start(bf16[4,2,8,1024]{3,2,1,0:T(8,128)(2,1)S(1)} %get-tuple-element.18), channel_id=1, source_target_pairs={{0,2},{1,3},{2,4},{3,5},{4,6},{5,7},{6,8},{7,9},{8,10},{9,11},{10,... | collective-permute-start | bytes 393224 | tf_op jit(solution)/shard_map/ppermute | solution.py:31
  160.0 8.6 %collective-permute-start.27 = (bf16[4,2,8,1024]{3,2,1,0:T(8,128)(2,1)S(1)}, bf16[4,2,8,1024]{3,2,1,0:T(8,128)(2,1)S(1)}, u32[]{:S(2)}, u32[]{:S(2)}) collective-permute-start(bf16[4,2,8,1024]{3,2,1,0:T(8,128)(2,1)S(1)} %get-tuple-element.18), channel_id=1, source_target_pairs={{0,62},{1,63},{2,0},{3,1},{4,2},{5,3},{6,4},{7,5},{8,6},{9,7},{10,... | collective-permute-start | bytes 393224 | tf_op jit(solution)/shard_map/ppermute | solution.py:31
  168.6 2.5 %copy-start.2 = (bf16[4,4,2,8,1024]{4,3,2,1,0:T(8,128)(2,1)}, bf16[4,4,2,8,1024]{4,3,2,1,0:T(8,128)(2,1)S(1)}, u32[]{:S(2)}) copy-start(bf16[4,4,2,8,1024]{4,3,2,1,0:T(8,128)(2,1)S(1)} %pad_maximum_fusion.1) | copy-start | bytes 1572868
  168.7 2.5 %collective-permute-start.28 = (bf16[4,4,2,8,1024]{4,3,2,1,0:T(8,128)(2,1)S(1)}, bf16[4,4,2,8,1024]{4,3,2,1,0:T(8,128)(2,1)S(1)}, u32[]{:S(2)}, u32[]{:S(2)}) collective-permute-start(bf16[4,4,2,8,1024]{4,3,2,1,0:T(8,128)(2,1)S(1)} %pad_maximum_fusion.1), channel_id=1, source_target_pairs={{0,1},{1,0},{2,3},{3,2},{4,5},{5,4},{6,7},{7,6},{8,9},{9,8},{10,11... | collective-permute-start | bytes 1572872 | tf_op jit(solution)/shard_map/ppermute | solution.py:43
  171.2 0.8 copy-start.4

commit v3 on v2

--- a/solution.py
+++ b/solution.py
@@ -16,6 +16,7 @@
 LANES = 128
 CHUNKS = 7
 VMEM_LIMIT = 55 * 1024 * 1024
+UNROLL = 4
 AXES = ("far", "near", "core")
 ALL = ("groups",) + AXES
 f32, bf16 = jnp.float32, jnp.bfloat16
@@ -47,15 +48,17 @@
     return jnp.where(lax.axis_index("core") == 0, first, second)
 
 
-def gathered(pair):
-    held = [pair]
-    for k in range(3):
+def gathered(pair, ready=None):
+    held = [pair, passed_on(pair)]
+    if ready is not None:
+        held[1], ready = lax.optimization_barrier((held[1], ready))
+    for k in range(2):
         held.append(passed_on(held[-1]))
     held[0] = of_core(pair, passed_on(held[-1], (1,)))
     far = jnp.stack(held)
     near = [far, along_z(far, (1, 1)), jnp.concatenate(two_away(far)), along_z(far, (-1, -1))]
     near = jnp.stack(near)
-    return near, other_core(near)
+    return near, other_core(near), ready
 
 
 def places(z, core, sign):
@@ -137,7 +140,7 @@
 
     for x, buf in enumerate((mine, theirs)):
 
-        @pl.loop(0, half)
+        @pl.loop(0, half, unroll=UNROLL)
         def _(i):
             device = order[0, x * half + i]
             heads[device // groups, lax.rem(device, groups)] = buf[i].astype(f32)
@@ -166,7 +169,7 @@
 
     for x, to in enumerate((kept, sent)):
 
-        @pl.loop(0, half)
+        @pl.loop(0, half, unroll=UNROLL)
         def _(i):
             device = order[1, x * half + i]
             q, g = device // groups, lax.rem(device, groups)
@@ -190,7 +193,7 @@
     dense[...] = jnp.zeros_like(dense)
     for x, buf in enumerate((mine, theirs)):
 
-        @pl.loop(0, half)
+        @pl.loop(0, half, unroll=UNROLL)
         def _(i):
             device = order[0, x * half + i]
             q, g = device // groups, lax.rem(device, groups)
@@ -234,7 +237,10 @@
     live_lengths = lax.dynamic_slice_in_dim(lengths, (me * entries) % ROWS, entries)
     attended = whole_attention(queries, keys, values, live_lengths, queries.shape[2] ** (-0.5))
     attended = attended.reshape(entries, -1)
-    mine, theirs = gathered(jnp.stack([attended, other_core(attended)]))
+    width = residual.shape[1]
+    ready = (order, residual, norm_gain.astype(f32).reshape(1, width))
+    mine, theirs, ready = gathered(jnp.stack([attended, other_core(attended)]), ready)
+    order, residual, gain = ready
 
     width = residual.shape[1]
     half = DEVICES // 2
@@ -267,7 +273,7 @@
         theirs.reshape(flat),
         residual,
         out_weight.T,
-        norm_gain.astype(f32).reshape(1, width),
+        gain,
         gate_weight,
         up_weight,
     )
@@ -279,7 +285,7 @@
     square_sums = jnp.sum(share[..., 2 * cols :], axis=-1, keepdims=True) / jnp.sum(weights)
     inverse = 1.0 / (square_sums / D + 1e-05)
     activated = jnp.maximum(share[..., :cols], 0.0) * share[..., cols : 2 * cols] * inverse
-    mine, theirs = gathered(activated.astype(bf16))
+    mine, theirs, _ = gathered(activated.astype(bf16))
 
     return pl.pallas_call(
         down_kernel,

time: 179 us -> 177 us (0.989)
  transfers between devices with their start and end apart: 29 -> 29, of which waited for: 19 -> 20; matrix products, arithmetic and copies ran while one was open for 2% -> 2% of each run, Pallas kernels for 0% -> 0%
where the time goes in v3:
time: 177 us; the launch traced here: 176 us
  waiting for transfers between devices  87.6 us (49%)
  starting transfers between devices  56.4 us (32%)
  Pallas kernels  17.4 us (10%)
  local copies, waits for them, and re-layouts  5.91 us (3%)
  other arithmetic  4.52 us (3%)
  matrix products  3.59 us (2%)
    ppermute x24, waiting for transfers between devices, along_z(): return lax.ppermute(x, AXES, pairs)  81.8 us
    ppermute x24, starting transfers between devices, along_z(): return lax.ppermute(x, AXES, pairs)  33.3 us
    ppermute x5, starting transfers between devices, other_core(): return lax.ppermute(x, 'core', [(0, 1), (1, 0)])  23.1 us
    pallas_call x1, Pallas kernels, body(): pl.pallas_call(up_kernel, in_specs=[SMEM, SMEM, VMEM, VMEM, VMEM, VMEM, V...  10.9 us
    pallas_call x1, Pallas kernels, body(): pl.pallas_call(down_kernel, in_specs=[SMEM, SMEM, VMEM, VMEM, VMEM, HBM],...  6.45 us
    ppermute x5, waiting for transfers between devices, other_core(): return lax.ppermute(x, 'core', [(0, 1), (1, 0)])  5.86 us
  transfers between devices with their start and end apart: 29, of which 20 were waited for; matrix products, arithmetic and copies ran while one was open for 2% of the time, Pallas kernels for 0%

profile of v3, /device:TPU:37, one launch (start us, length us, event | category | flops | bytes accessed | tf_op | source)
XLA Modules:
  0.0 175.8 jit_solution(15476195468720534784)
XLA Ops:
  0.0 0.9 dynamic_slice.7
  1.0 0.6 copy-done
  1.6 1.6 fusion.29
  3.2 2.0 %convolution_convert_fusion = bf16[8,8,128]{2,1,0:T(8,128)(2,1)S(1)} fusion(bf16[8,1024,128]{2,1,0:T(8,128)(2,1)} %param.14, f32[8,8,1024]{2,1,0:T(8,128)S(1)} %get-tuple-element.34, f32[8,8]{1,0:T(8,128)S(1)} %get-tuple-element.33), kind=kOutput, calls=%fused_computation.7 | convolution fusion | flops 16916480 | bytes 2375936 | tf_op jit(solution)/shard_map/egt,etc->egc/dot_general | solution.py:113
  5.2 20.5 %collective-permute-start = (bf16[8,1024]{1,0:T(8,128)(2,1)S(1)}, bf16[8,1024]{1,0:T(8,128)(2,1)S(1)}, u32[]{:S(2)}, u32[]{:S(2)}) collective-permute-start(bf16[8,1024]{1,0:T(8,128)(2,1)S(1)} %bitcast.186), channel_id=1, source_target_pairs={{0,1},{1,0},{2,3},{3,2},{4,5},{5,4},{6,7},{7,6},{8,9},{9,8},{10,11... | collective-permute-start | bytes 49160 | tf_op jit(solution)/shard_map/ppermute | solution.py:44
  25.8 0.5 bitcast_convert_fusion.gain
  26.6 1.3 dynamic-slice_bitcast_fusion.order
  27.9 5.4 %collective-permute-done.1 = bf16[2,8,1024]{2,1,0:T(8,128)(2,1)S(1)} collective-permute-done((bf16[2,8,1024]{2,1,0:T(8,128)(2,1)S(1)}, bf16[2,8,1024]{2,1,0:T(8,128)(2,1)S(1)}, u32[]{:S(2)}, u32[]{:S(2)}) %collective-permute-start.1) | collective-permute-done | bytes 32800 | tf_op jit(solution)/shard_map/ppermute | solution.py:32
  33.3 6.8 %collective-permute-done.2 = bf16[2,8,1024]{2,1,0:T(8,128)(2,1)S(1)} collective-permute-done((bf16[2,8,1024]{2,1,0:T(8,128)(2,1)S(1)}, bf16[2,8,1024]{2,1,0:T(8,128)(2,1)S(1)}, u32[]{:S(2)}, u32[]{:S(2)}) %collective-permute-start.2) | collective-permute-done | bytes 32800 | tf_op jit(solution)/shard_map/ppermute | solution.py:32
  40.1 6.8 %collective-permute-done.3 = bf16[2,8,1024]{2,1,0:T(8,128)(2,1)S(1)} collective-permute-done((bf16[2,8,1024]{2,1,0:T(8,128)(2,1)S(1)}, bf16[2,8,1024]{2,1,0:T(8,128)(2,1)S(1)}, u32[]{:S(2)}, u32[]{:S(2)}) %collective-permute-start.3) | collective-permute-done | bytes 32800 | tf_op jit(solution)/shard_map/ppermute | solution.py:32
  46.8 1.9 %collective-permute-start.4 = (bf16[2,8,1024]{2,1,0:T(8,128)(2,1)S(1)}, bf16[2,8,1024]{2,1,0:T(8,128)(2,1)S(1)}, u32[]{:S(2)}, u32[]{:S(2)}) collective-permute-start(bf16[2,8,1024]{2,1,0:T(8,128)(2,1)S(1)} %collective-permute-done.3), channel_id=1, source_target_pairs={{1,9},{3,11},{5,13},{7,15},{9,17},{11,19},{13,21},{15,23},{17,25},... | collective-permute-start | bytes 98312 | tf_op jit(solution)/shard_map/ppermute | solution.py:32
  48.8 2.7 %collective-permute-start.6 = (bf16[2,2,8,1024]{3,2,1,0:T(8,128)(2,1)S(1)}, bf16[2,2,8,1024]{3,2,1,0:T(8,128)(2,1)S(1)}, u32[]{:S(2)}, u32[]{:S(2)}) collective-permute-start(bf16[2,2,8,1024]{3,2,1,0:T(8,128)(2,1)S(1)} %get-tuple-element.31), channel_id=1, source_target_pairs={{0,60},{1,5},{2,62},{3,7},{4,0},{5,9},{6,2},{7,11},{8,4},{9,13},{1... | collective-permute-start | bytes 196616 | tf_op jit(solution)/shard_map/ppermute | solution.py:32
  51.5 3.3 %collective-permute-start.7 = (bf16[2,2,8,1024]{3,2,1,0:T(8,128)(2,1)S(1)}, bf16[2,2,8,1024]{3,2,1,0:T(8,128)(2,1)S(1)}, u32[]{:S(2)}, u32[]{:S(2)}) collective-permute-start(bf16[2,2,8,1024]{3,2,1,0:T(8,128)(2,1)S(1)} %get-tuple-element.32), channel_id=1, source_target_pairs={{0,4},{1,61},{2,6},{3,63},{4,8},{5,1},{6,10},{7,3},{8,12},{9,5},{1... | collective-permute-start | bytes 196616 | tf_op jit(solution)/shard_map/ppermute | solution.py:32
  54.8 0.6 collective-permute-done.4
  55.5 1.6 collective-permute-start.5
  57.1 5.2 %collective-permute-start.8 = (bf16[4,2,8,1024]{3,2,1,0:T(8,128)(2,1)S(1)}, bf16[4,2,8,1024]{3,2,1,0:T(8,128)(2,1)S(1)}, u32[]{:S(2)}, u32[]{:S(2)}) collective-permute-start(bf16[4,2,8,1024]{3,2,1,0:T(8,128)(2,1)S(1)} %get-tuple-element.28), channel_id=1, source_target_pairs={{0,62},{1,63},{2,0},{3,1},{4,2},{5,3},{6,4},{7,5},{8,6},{9,7},{10,... | collective-permute-start | bytes 393224 | tf_op jit(solution)/shard_map/ppermute | solution.py:32
  62.3 2.2 %collective-permute-done.5 = bf16[4,2,8,1024]{3,2,1,0:T(8,128)(2,1)S(1)} collective-permute-done((bf16[4,2,8,1024]{3,2,1,0:T(8,128)(2,1)S(1)}, bf16[4,2,8,1024]{3,2,1,0:T(8,128)(2,1)S(1)}, u32[]{:S(2)}, u32[]{:S(2)}) %collective-permute-start.5) | collective-permute-done | bytes 131104 | tf_op jit(solution)/shard_map/ppermute | solution.py:32
  64.8 0.7 copy.13.residual
  65.5 1.1 collective-permute-done.9
  66.7 0.8 copy-done.3
  67.5 10.9 %up_kernel.1 = (f32[128,64]{1,0:T(8,128)}, f32[32,8,2176]{2,1,0:T(8,128)}, bf16[32,8,2176]{2,1,0:T(8,128)(2,1)}) custom-call(s32[2,64]{1,0:T(2,128)} %dynamic-slice_bitcast_fusion.order, s32[16,32]{1,0:T(8,128)} %active.3, bf16[32,8,1024]{2,1,0:T(8,128)(2,1)} %bitcast.160, bf16[32,8,1024]{2,1,0:T(8,128)(2,1)} %bitcast.164, bf16[128,64]{1,0:T(8,128)(2,1)} %copy.13.residual, ...), custom_call_target="tpu_custom_call" | custom-call | tf_op jit(solution)/shard_map/up_kernel/pallas_call | solution.py:250
  78.9 2.8 %collective-permute-done.10 = bf16[4,4,2,8,2176]{4,3,2,1,0:T(8,128)(2,1)S(1)} collective-permute-done((bf16[4,4,2,8,2176]{4,3,2,1,0:T(8,128)(2,1)}, bf16[4,4,2,8,2176]{4,3,2,1,0:T(8,128)(2,1)S(1)}, u32[]{:S(2)}, u32[]{:S(2)}) %collective-permute-start.10) | collective-permute-done | bytes 1114144 | tf_op jit(solution)/shard_map/ppermute | solution.py:44
  81.7 1.9 %fusion.28 = (bf16[4,4,2,8,2176]{4,3,2,1,0:T(8,128)(2,1)S(1)}, f32[4,4,2,8,2176]{4,3,2,1,0:T(8,128)S(1)}) fusion(f32[4,4,2,8,2176]{4,3,2,1,0:T(8,128)} %bitcast.159, bf16[4,4,2,8,2176]{4,3,2,1,0:T(8,128)(2,1)S(1)} %collective-permute-done.10), kind=kLoop, calls=%fused_computation.74 | loop fusion | flops 1671168 | bytes 6684672 | tf_op jit(solution)/shard_map/convert_element_type | solution.py:86
  83.8 2.9 %collective-permute-start.12 = (bf16[4,2,8,2176]{3,2,1,0:T(8,128)(2,1)S(1)}, bf16[4,2,8,2176]{3,2,1,0:T(8,128)(2,1)S(1)}, u32[]{:S(2)}, u32[]{:S(2)}) collective-permute-start(bf16[4,2,8,2176]{3,2,1,0:T(8,128)(2,1)S(1)} %get-tuple-element.24), channel_id=1, source_target_pairs={{0,62},{1,63},{2,0},{3,1},{4,2},{5,3},{6,4},{7,5},{8,6},{9,7},{10,... | collective-permute-start | bytes 835592 | tf_op jit(solution)/shard_map/ppermute | solution.py:32
  86.9 6.5 %collective-permute-done.11 = bf16[4,2,8,2176]{3,2,1,0:T(8,128)(2,1)S(1)} collective-permute-done((bf16[4,2,8,2176]{3,2,1,0:T(8,128)(2,1)S(1)}, bf16[4,2,8,2176]{3,2,1,0:T(8,128)(2,1)S(1)}, u32[]{:S(2)}, u32[]{:S(2)}) %collective-permute-start.11) | collective-permute-done | bytes 278560 | tf_op jit(solution)/shard_map/ppermute | solution.py:32
  93.4 2.7 %collective-permute-start.13 = (bf16[2,8,2176]{2,1,0:T(8,128)(2,1)S(1)}, bf16[2,8,2176]{2,1,0:T(8,128)(2,1)S(1)}, u32[]{:S(2)}, u32[]{:S(2)}) collective-permute-start(bf16[2,8,2176]{2,1,0:T(8,128)(2,1)S(1)} %fusion.25), channel_id=1, source_target_pairs={{1,9},{3,11},{5,13},{7,15},{9,17},{11,19},{13,21},{15,23},{17,25},... | collective-permute-start | bytes 208904 | tf_op jit(solution)/shard_map/ppermute | solution.py:32
  96.1 2.3 %collective-permute-start.16 = (bf16[2,2,8,2176]{3,2,1,0:T(8,128)(2,1)S(1)}, bf16[2,2,8,2176]{3,2,1,0:T(8,128)(2,1)S(1)}, u32[]{:S(2)}, u32[]{:S(2)}) collective-permute-start(bf16[2,2,8,2176]{3,2,1,0:T(8,128)(2,1)S(1)} %get-tuple-element.21), channel_id=1, source_target_pairs={{0,4},{1,61},{2,6},{3,63},{4,8},{5,1},{6,10},{7,3},{8,12},{9,5},{1... | collective-permute-start | bytes 417800 | tf_op jit(solution)/shard_map/ppermute | solution.py:32
  98.4 7.2 %collective-permute-done.13 = bf16[2,8,2176]{2,1,0:T(8,128)(2,1)S(1)} collective-permute-done((bf16[2,8,2176]{2,1,0:T(8,128)(2,1)S(1)}, bf16[2,8,2176]{2,1,0:T(8,128)(2,1)S(1)}, u32[]{:S(2)}, u32[]{:S(2)}) %collective-permute-start.13) | collective-permute-done | bytes 69664 | tf_op jit(solution)/shard_map/ppermute | solution.py:32
  105.8 7.3 %collective-permute-done.15 = bf16[2,8,2176]{2,1,0:T(8,128)(2,1)S(1)} collective-permute-done((bf16[2,8,2176]{2,1,0:T(8,128)(2,1)S(1)}, bf16[2,8,2176]{2,1,0:T(8,128)(2,1)S(1)}, u32[]{:S(2)}, u32[]{:S(2)}) %collective-permute-start.15) | collective-permute-done | bytes 69664 | tf_op jit(solution)/shard_map/ppermute | solution.py:32
  113.2 7.1 %collective-permute-done.17 = bf16[2,8,2176]{2,1,0:T(8,128)(2,1)S(1)} collective-permute-done((bf16[2,8,2176]{2,1,0:T(8,128)(2,1)S(1)}, bf16[2,8,2176]{2,1,0:T(8,128)(2,1)S(1)}, u32[]{:S(2)}, u32[]{:S(2)}) %collective-permute-start.17) | collective-permute-done | bytes 69664 | tf_op jit(solution)/shard_map/ppermute | solution.py:32
  120.5 7.1 %collective-permute-done.18 = bf16[2,8,2176]{2,1,0:T(8,128)(2,1)S(1)} collective-permute-done((bf16[2,8,2176]{2,1,0:T(8,128)(2,1)S(1)}, bf16[2,8,2176]{2,1,0:T(8,128)(2,1)S(1)}, u32[]{:S(2)}, u32[]{:S(2)}) %collective-permute-start.18) | collective-permute-done | bytes 69664 | tf_op jit(solution)/shard_map/ppermute | solution.py:32
  127.7 0.6 add_reduce_fusion
  128.3 0.7 collective-permute-done.19
  129.1 0.7 add_divide_fusion
  130.0 6.6 %collective-permute-done.20 = bf16[2,8,1024]{2,1,0:T(8,128)(2,1)S(1)} collective-permute-done((bf16[2,8,1024]{2,1,0:T(8,128)(2,1)S(1)}, bf16[2,8,1024]{2,1,0:T(8,128)(2,1)S(1)}, u32[]{:S(2)}, u32[]{:S(2)}) %collective-permute-start.20) | collective-permute-done | bytes 32800 | tf_op jit(solution)/shard_map/ppermute | solution.py:32
  136.7 6.6 %collective-permute-done.21 = bf16[2,8,1024]{2,1,0:T(8,128)(2,1)S(1)} collective-permute-done((bf16[2,8,1024]{2,1,0:T(8,128)(2,1)S(1)}, bf16[2,8,1024]{2,1,0:T(8,128)(2,1)S(1)}, u32[]{:S(2)}, u32[]{:S(2)}) %collective-permute-start.21) | collective-permute-done | bytes 32800 | tf_op jit(solution)/shard_map/ppermute | solution.py:32
  143.3 6.6 %collective-permute-done.22 = bf16[2,8,1024]{2,1,0:T(8,128)(2,1)S(1)} collective-permute-done((bf16[2,8,1024]{2,1,0:T(8,128)(2,1)S(1)}, bf16[2,8,1024]{2,1,0:T(8,128)(2,1)S(1)}, u32[]{:S(2)}, u32[]{:S(2)}) %collective-permute-start.22) | collective-permute-done | bytes 32800 | tf_op jit(solution)/shard_map/ppermute | solution.py:32
  150.0 2.0 %collective-permute-start.23 = (bf16[2,8,1024]{2,1,0:T(8,128)(2,1)S(1)}, bf16[2,8,1024]{2,1,0:T(8,128)(2,1)S(1)}, u32[]{:S(2)}, u32[]{:S(2)}) collective-permute-start(bf16[2,8,1024]{2,1,0:T(8,128)(2,1)S(1)} %collective-permute-done.22), channel_id=1, source_target_pairs={{1,9},{3,11},{5,13},{7,15},{9,17},{11,19},{13,21},{15,23},{17,25},... | collective-permute-start | bytes 98312 | tf_op jit(solution)/shard_map/ppermute | solution.py:32
  152.0 4.9 %collective-permute-start.25 = (bf16[2,2,8,1024]{3,2,1,0:T(8,128)(2,1)S(1)}, bf16[2,2,8,1024]{3,2,1,0:T(8,128)(2,1)S(1)}, u32[]{:S(2)}, u32[]{:S(2)}) collective-permute-start(bf16[2,2,8,1024]{3,2,1,0:T(8,128)(2,1)S(1)} %get-tuple-element.29), channel_id=1, source_target_pairs={{0,60},{1,5},{2,62},{3,7},{4,0},{5,9},{6,2},{7,11},{8,4},{9,13},{1... | collective-permute-start | bytes 196616 | tf_op jit(solution)/shard_map/ppermute | solution.py:32
  156.9 1.7 collective-permute-done.23
  158.6 1.1 collective-permute-start.24
  159.7 1.7 collective-permute-start.27
  161.5 3.5 %collective-permute-done.24 = bf16[4,2,8,1024]{3,2,1,0:T(8,128)(2,1)S(1)} collective-permute-done((bf16[4,2,8,1024]{3,2,1,0:T(8,128)(2,1)S(1)}, bf16[4,2,8,1024]{3,2,1,0:T(8,128)(2,1)S(1)}, u32[]{:S(2)}, u32[]{:S(2)}) %collective-permute-start.24) | collective-permute-done | bytes 131104 | tf_op jit(solution)/shard_map/ppermute | solution.py:32
  165.0 1.8 %collective-permute-start.28 = (bf16[4,4,2,8,1024]{4,3,2,1,0:T(8,128)(2,1)S(1)}, bf16[4,4,2,8,1024]{4,3,2,1,0:T(8,128)(2,1)S(1)}, u32[]{:S(2)}, u32[]{:S(2)}) collective-permute-start(bf16[4,4,2,8,1024]{4,3,2,1,0:T(8,128)(2,1)S(1)} %pad_maximum_fusion.1), channel_id=1, source_target_pairs={{0,1},{1,0},{2,3},{3,2},{4,5},{5,4},{6,7},{7,6},{8,9},{9,8},{10,11... | collective-permute-start | bytes 1572872 | tf_op jit(solution)/shard_map/ppermute | solution.py:44
  166.9 0.7 copy.14
  167.5 0.8 collective-permute-done.28
  168.4 0.8 copy-done.4
  169.2 6.4 %down_kernel.1 = bf16[64,128]{1,0:T(8,128)(2,1)} custom-call(s32[2,64]{1,0:T(2,128)} %dynamic-slice_bitcast_fusion.order, s32[16,32]{1,0:T(8,128)} %active.3, bf16[32,8,1024]{2,1,0:T(8,128)(2,1)} %bitcast.161, bf16[32,8,1024]{2,1,0:T(8,128)(2,1)} %bitcast.165, f32[64,128]{1,0:T(8,128)} %bitcast.167, bf16[64,14336]{1,0:T(8,128)(2,1)} %bitcast.162), custom_call_target="tpu_custom_call" | custom-call | tf_op jit(solution)/shard_map/down_kernel/pallas_call | solution.py:290
  (62 shorter events, 2.9 us)
Async XLA Ops:
  0.0 1.6 copy-start
  1.6 24.2 %copy-start.7 = (bf16[64]{0:T(256)(128)(2,1)S(1)}, bf16[64]{0:T(256)(128)(2,1)}, u32[]{:S(2)}) copy-start(bf16[64]{0:T(256)(128)(2,1)} %param.19) | copy-start | bytes 388
  3.2 61.6 %copy-start.6 = (bf16[128,64]{0,1:T(8,128)(2,1)S(1)}, bf16[128,64]{0,1:T(8,128)(2,1)}, u32[]{:S(2)}) copy-start(bf16[128,64]{0,1:T(8,128)(2,1)} %param.17) | copy-start | bytes 49156
  5.2 21.4 %collective-permute-start = (bf16[8,1024]{1,0:T(8,128)(2,1)S(1)}, bf16[8,1024]{1,0:T(8,128)(2,1)S(1)}, u32[]{:S(2)}, u32[]{:S(2)}) collective-permute-start(bf16[8,1024]{1,0:T(8,128)(2,1)S(1)} %bitcast.186), channel_id=1, source_target_pairs={{0,1},{1,0},{2,3},{3,2},{4,5},{5,4},{6,7},{7,6},{8,9},{9,8},{10,11... | collective-permute-start | bytes 49160 | tf_op jit(solution)/shard_map/ppermute | solution.py:44
  26.6 6.7 %collective-permute-start.1 = (bf16[2,8,1024]{2,1,0:T(8,128)(2,1)S(1)}, bf16[2,8,1024]{2,1,0:T(8,128)(2,1)S(1)}, u32[]{:S(2)}, u32[]{:S(2)}) collective-permute-start(bf16[2,8,1024]{2,1,0:T(8,128)(2,1)S(1)} %pad_maximum_fusion.8), channel_id=1, source_target_pairs={{0,56},{1,9},{2,58},{3,11},{4,60},{5,13},{6,62},{7,15},{8,0},{9,17... | collective-permute-start | bytes 98312 | tf_op jit(solution)/shard_map/ppermute | solution.py:32
  33.3 6.8 %collective-permute-start.2 = (bf16[2,8,1024]{2,1,0:T(8,128)(2,1)S(1)}, bf16[2,8,1024]{2,1,0:T(8,128)(2,1)S(1)}, u32[]{:S(2)}, u32[]{:S(2)}) collective-permute-start(bf16[2,8,1024]{2,1,0:T(8,128)(2,1)S(1)} %collective-permute-done.1), channel_id=1, source_target_pairs={{0,56},{1,9},{2,58},{3,11},{4,60},{5,13},{6,62},{7,15},{8,0},{9,17... | collective-permute-start | bytes 98312 | tf_op jit(solution)/shard_map/ppermute | solution.py:32
  40.1 6.8 %collective-permute-start.3 = (bf16[2,8,1024]{2,1,0:T(8,128)(2,1)S(1)}, bf16[2,8,1024]{2,1,0:T(8,128)(2,1)S(1)}, u32[]{:S(2)}, u32[]{:S(2)}) collective-permute-start(bf16[2,8,1024]{2,1,0:T(8,128)(2,1)S(1)} %collective-permute-done.2), channel_id=1, source_target_pairs={{0,56},{1,9},{2,58},{3,11},{4,60},{5,13},{6,62},{7,15},{8,0},{9,17... | collective-permute-start | bytes 98312 | tf_op jit(solution)/shard_map/ppermute | solution.py:32
  46.8 8.6 %collective-permute-start.4 = (bf16[2,8,1024]{2,1,0:T(8,128)(2,1)S(1)}, bf16[2,8,1024]{2,1,0:T(8,128)(2,1)S(1)}, u32[]{:S(2)}, u32[]{:S(2)}) collective-permute-start(bf16[2,8,1024]{2,1,0:T(8,128)(2,1)S(1)} %collective-permute-done.3), channel_id=1, source_target_pairs={{1,9},{3,11},{5,13},{7,15},{9,17},{11,19},{13,21},{15,23},{17,25},... | collective-permute-start | bytes 98312 | tf_op jit(solution)/shard_map/ppermute | solution.py:32
  48.8 13.5 %collective-permute-start.6 = (bf16[2,2,8,1024]{3,2,1,0:T(8,128)(2,1)S(1)}, bf16[2,2,8,1024]{3,2,1,0:T(8,128)(2,1)S(1)}, u32[]{:S(2)}, u32[]{:S(2)}) collective-permute-start(bf16[2,2,8,1024]{3,2,1,0:T(8,128)(2,1)S(1)} %get-tuple-element.31), channel_id=1, source_target_pairs={{0,60},{1,5},{2,62},{3,7},{4,0},{5,9},{6,2},{7,11},{8,4},{9,13},{1... | collective-permute-start | bytes 196616 | tf_op jit(solution)/shard_map/ppermute | solution.py:32
  51.5 10.8 %collective-permute-start.7 = (bf16[2,2,8,1024]{3,2,1,0:T(8,128)(2,1)S(1)}, bf16[2,2,8,1024]{3,2,1,0:T(8,128)(2,1)S(1)}, u32[]{:S(2)}, u32[]{:S(2)}) collective-permute-start(bf16[2,2,8,1024]{3,2,1,0:T(8,128)(2,1)S(1)} %get-tuple-element.32), channel_id=1, source_target_pairs={{0,4},{1,61},{2,6},{3,63},{4,8},{5,1},{6,10},{7,3},{8,12},{9,5},{1... | collective-permute-start | bytes 196616 | tf_op jit(solution)/shard_map/ppermute | solution.py:32
  55.5 9.1 %collective-permute-start.5 = (bf16[4,2,8,1024]{3,2,1,0:T(8,128)(2,1)S(1)}, bf16[4,2,8,1024]{3,2,1,0:T(8,128)(2,1)S(1)}, u32[]{:S(2)}, u32[]{:S(2)}) collective-permute-start(bf16[4,2,8,1024]{3,2,1,0:T(8,128)(2,1)S(1)} %get-tuple-element.28), channel_id=1, source_target_pairs={{0,2},{1,3},{2,4},{3,5},{4,6},{5,7},{6,8},{7,9},{8,10},{9,11},{10,... | collective-permute-start | bytes 393224 | tf_op jit(solution)/shard_map/ppermute | solution.py:32
  57.1 7.4 %collective-permute-start.8 = (bf16[4,2,8,1024]{3,2,1,0:T(8,128)(2,1)S(1)}, bf16[4,2,8,1024]{3,2,1,0:T(8,128)(2,1)S(1)}, u32[]{:S(2)}, u32[]{:S(2)}) collective-permute-start(bf16[4,2,8,1024]{3,2,1,0:T(8,128)(2,1)S(1)} %get-tuple-element.28), channel_id=1, source_target_pairs={{0,62},{1,63},{2,0},{3,1},{4,2},{5,3},{6,4},{7,5},{8,6},{9,7},{10,... | collective-permute-start | bytes 393224 | tf_op jit(solution)/shard_map/ppermute | solution.py:32
  64.6 2.0 %copy-start.1 = (bf16[4,4,2,8,1024]{4,3,2,1,0:T(8,128)(2,1)}, bf16[4,4,2,8,1024]{4,3,2,1,0:T(8,128)(2,1)S(1)}, u32[]{:S(2)}) copy-start(bf16[4,4,2,8,1024]{4,3,2,1,0:T(8,128)(2,1)S(1)} %pad_maximum_fusion) | copy-start | bytes 1572868
  64.6 2.0 %collective-permute-start.9 = (bf16[4,4,2,8,1024]{4,3,2,1,0:T(8,128)(2,1)S(1)}, bf16[4,4,2,8,1024]{4,3,2,1,0:T(8,128)(2,1)S(1)}, u32[]{:S(2)}, u32[]{:S(2)}) collective-permute-start(bf16[4,4,2,8,1024]{4,3,2,1,0:T(8,128)(2,1)S(1)} %pad_maximum_fusion), channel_id=1, source_target_pairs={{0,1},{1,0},{2,3},{3,2},{4,5},{5,4},{6,7},{7,6},{8,9},{9,8},{10,11... | collective-permute-start | bytes 1572872 | tf_op jit(solution)/shard_map/ppermute | solution.py:44
  66.7 0.8 copy-start.3
  78.4 3.3 %collective-permute-start.10 = (bf16[4,4,2,8,2176]{4,3,2,1,0:T(8,128)(2,1)}, bf16[4,4,2,8,2176]{4,3,2,1,0:T(8,128)(2,1)S(1)}, u32[]{:S(2)}, u32[]{:S(2)}) collective-permute-start(bf16[4,4,2,8,2176]{4,3,2,1,0:T(8,128)(2,1)} %bitcast.187), channel_id=1, source_target_pairs={{0,1},{1,0},{2,3},{3,2},{4,5},{5,4},{6,7},{7,6},{8,9},{9,8},{10,11... | collective-permute-start | bytes 3342344 | tf_op jit(solution)/shard_map/ppermute | solution.py:44
  83.7 9.7 %collective-permute-start.11 = (bf16[4,2,8,2176]{3,2,1,0:T(8,128)(2,1)S(1)}, bf16[4,2,8,2176]{3,2,1,0:T(8,128)(2,1)S(1)}, u32[]{:S(2)}, u32[]{:S(2)}) collective-permute-start(bf16[4,2,8,2176]{3,2,1,0:T(8,128)(2,1)S(1)} %get-tuple-element.23), channel_id=1, source_target_pairs={{0,2},{1,3},{2,4},{3,5},{4,6},{5,7},{6,8},{7,9},{8,10},{9,11},{10,... | collective-permute-start | bytes 835592 | tf_op jit(solution)/shard_map/ppermute | solution.py:32
  83.8 9.5 %collective-permute-start.12 = (bf16[4,2,8,2176]{3,2,1,0:T(8,128)(2,1)S(1)}, bf16[4,2,8,2176]{3,2,1,0:T(8,128)(2,1)S(1)}, u32[]{:S(2)}, u32[]{:S(2)}) collective-permute-start(bf16[4,2,8,2176]{3,2,1,0:T(8,128)(2,1)S(1)} %get-tuple-element.24), channel_id=1, source_target_pairs={{0,62},{1,63},{2,0},{3,1},{4,2},{5,3},{6,4},{7,5},{8,6},{9,7},{10,... | collective-permute-start | bytes 835592 | tf_op jit(solution)/shard_map/ppermute | solution.py:32
  86.8 11.6 %collective-permute-start.14 = (bf16[2,2,8,2176]{3,2,1,0:T(8,128)(2,1)S(1)}, bf16[2,2,8,2176]{3,2,1,0:T(8,128)(2,1)S(1)}, u32[]{:S(2)}, u32[]{:S(2)}) collective-permute-start(bf16[2,2,8,2176]{3,2,1,0:T(8,128)(2,1)S(1)} %get-tuple-element.22), channel_id=1, source_target_pairs={{0,60},{1,5},{2,62},{3,7},{4,0},{5,9},{6,2},{7,11},{8,4},{9,13},{1... | collective-permute-start | bytes 417800 | tf_op jit(solution)/shard_map/ppermute | solution.py:32
  93.4 12.2 %collective-permute-start.13 = (bf16[2,8,2176]{2,1,0:T(8,128)(2,1)S(1)}, bf16[2,8,2176]{2,1,0:T(8,128)(2,1)S(1)}, u32[]{:S(2)}, u32[]{:S(2)}) collective-permute-start(bf16[2,8,2176]{2,1,0:T(8,128)(2,1)S(1)} %fusion.25), channel_id=1, source_target_pairs={{1,9},{3,11},{5,13},{7,15},{9,17},{11,19},{13,21},{15,23},{17,25},... | collective-permute-start | bytes 208904 | tf_op jit(solution)/shard_map/ppermute | solution.py:32
  96.1 9.7 %collective-permute-start.16 = (bf16[2,2,8,2176]{3,2,1,0:T(8,128)(2,1)S(1)}, bf16[2,2,8,2176]{3,2,1,0:T(8,128)(2,1)S(1)}, u32[]{:S(2)}, u32[]{:S(2)}) collective-permute-start(bf16[2,2,8,2176]{3,2,1,0:T(8,128)(2,1)S(1)} %get-tuple-element.21), channel_id=1, source_target_pairs={{0,4},{1,61},{2,6},{3,63},{4,8},{5,1},{6,10},{7,3},{8,12},{9,5},{1... | collective-permute-start | bytes 417800 | tf_op jit(solution)/shard_map/ppermute | solution.py:32
  105.6 61.3 %copy-start.5 = (f32[128,64]{1,0:T(8,128)S(1)}, f32[128,64]{1,0:T(8,128)}, u32[]{:S(2)}) copy-start(f32[128,64]{1,0:T(8,128)} %get-tuple-element.18) | copy-start | bytes 98308
  105.6 7.4 %collective-permute-start.15 = (bf16[2,8,2176]{2,1,0:T(8,128)(2,1)S(1)}, bf16[2,8,2176]{2,1,0:T(8,128)(2,1)S(1)}, u32[]{:S(2)}, u32[]{:S(2)}) collective-permute-start(bf16[2,8,2176]{2,1,0:T(8,128)(2,1)S(1)} %fusion.19), channel_id=1, source_target_pairs={{0,56},{1,9},{2,58},{3,11},{4,60},{5,13},{6,62},{7,15},{8,0},{9,17... | collective-permute-start | bytes 208904 | tf_op jit(solution)/shard_map/ppermute | solution.py:32
  113.1 7.2 %collective-permute-start.17 = (bf16[2,8,2176]{2,1,0:T(8,128)(2,1)S(1)}, bf16[2,8,2176]{2,1,0:T(8,128)(2,1)S(1)}, u32[]{:S(2)}, u32[]{:S(2)}) collective-permute-start(bf16[2,8,2176]{2,1,0:T(8,128)(2,1)S(1)} %fusion.14), channel_id=1, source_target_pairs={{0,56},{1,9},{2,58},{3,11},{4,60},{5,13},{6,62},{7,15},{8,0},{9,17... | collective-permute-start | bytes 208904 | tf_op jit(solution)/shard_map/ppermute | solution.py:32
  120.3 7.2 %collective-permute-start.18 = (bf16[2,8,2176]{2,1,0:T(8,128)(2,1)S(1)}, bf16[2,8,2176]{2,1,0:T(8,128)(2,1)S(1)}, u32[]{:S(2)}, u32[]{:S(2)}) collective-permute-start(bf16[2,8,2176]{2,1,0:T(8,128)(2,1)S(1)} %fusion.9), channel_id=1, source_target_pairs={{0,56},{1,9},{2,58},{3,11},{4,60},{5,13},{6,62},{7,15},{8,0},{9,17... | collective-permute-start | bytes 208904 | tf_op jit(solution)/shard_map/ppermute | solution.py:32
  127.5 1.5 collective-permute-start.19
  129.9 6.7 %collective-permute-start.20 = (bf16[2,8,1024]{2,1,0:T(8,128)(2,1)S(1)}, bf16[2,8,1024]{2,1,0:T(8,128)(2,1)S(1)}, u32[]{:S(2)}, u32[]{:S(2)}) collective-permute-start(bf16[2,8,1024]{2,1,0:T(8,128)(2,1)S(1)} %fusion.24), channel_id=1, source_target_pairs={{0,56},{1,9},{2,58},{3,11},{4,60},{5,13},{6,62},{7,15},{8,0},{9,17... | collective-permute-start | bytes 98312 | tf_op jit(solution)/shard_map/ppermute | solution.py:32
  136.6 6.7 %collective-permute-start.21 = (bf16[2,8,1024]{2,1,0:T(8,128)(2,1)S(1)}, bf16[2,8,1024]{2,1,0:T(8,128)(2,1)S(1)}, u32[]{:S(2)}, u32[]{:S(2)}) collective-permute-start(bf16[2,8,1024]{2,1,0:T(8,128)(2,1)S(1)} %collective-permute-done.20), channel_id=1, source_target_pairs={{0,56},{1,9},{2,58},{3,11},{4,60},{5,13},{6,62},{7,15},{8,0},{9,17... | collective-permute-start | bytes 98312 | tf_op jit(solution)/shard_map/ppermute | solution.py:32
  143.3 6.7 %collective-permute-start.22 = (bf16[2,8,1024]{2,1,0:T(8,128)(2,1)S(1)}, bf16[2,8,1024]{2,1,0:T(8,128)(2,1)S(1)}, u32[]{:S(2)}, u32[]{:S(2)}) collective-permute-start(bf16[2,8,1024]{2,1,0:T(8,128)(2,1)S(1)} %collective-permute-done.21), channel_id=1, source_target_pairs={{0,56},{1,9},{2,58},{3,11},{4,60},{5,13},{6,62},{7,15},{8,0},{9,17... | collective-permute-start | bytes 98312 | tf_op jit(solution)/shard_map/ppermute | solution.py:32
  150.0 8.6 %collective-permute-start.23 = (bf16[2,8,1024]{2,1,0:T(8,128)(2,1)S(1)}, bf16[2,8,1024]{2,1,0:T(8,128)(2,1)S(1)}, u32[]{:S(2)}, u32[]{:S(2)}) collective-permute-start(bf16[2,8,1024]{2,1,0:T(8,128)(2,1)S(1)} %collective-permute-done.22), channel_id=1, source_target_pairs={{1,9},{3,11},{5,13},{7,15},{9,17},{11,19},{13,21},{15,23},{17,25},... | collective-permute-start | bytes 98312 | tf_op jit(solution)/shard_map/ppermute | solution.py:32
  152.0 9.5 %collective-permute-start.25 = (bf16[2,2,8,1024]{3,2,1,0:T(8,128)(2,1)S(1)}, bf16[2,2,8,1024]{3,2,1,0:T(8,128)(2,1)S(1)}, u32[]{:S(2)}, u32[]{:S(2)}) collective-permute-start(bf16[2,2,8,1024]{3,2,1,0:T(8,128)(2,1)S(1)} %get-tuple-element.29), channel_id=1, source_target_pairs={{0,60},{1,5},{2,62},{3,7},{4,0},{5,9},{6,2},{7,11},{8,4},{9,13},{1... | collective-permute-start | bytes 196616 | tf_op jit(solution)/shard_map/ppermute | solution.py:32
  156.9 4.6 %collective-permute-start.26 = (bf16[2,2,8,1024]{3,2,1,0:T(8,128)(2,1)S(1)}, bf16[2,2,8,1024]{3,2,1,0:T(8,128)(2,1)S(1)}, u32[]{:S(2)}, u32[]{:S(2)}) collective-permute-start(bf16[2,2,8,1024]{3,2,1,0:T(8,128)(2,1)S(1)} %get-tuple-element.30), channel_id=1, source_target_pairs={{0,4},{1,61},{2,6},{3,63},{4,8},{5,1},{6,10},{7,3},{8,12},{9,5},{1... | collective-permute-start | bytes 196616 | tf_op jit(solution)/shard_map/ppermute | solution.py:32
  158.6 6.3 %collective-permute-start.24 = (bf16[4,2,8,1024]{3,2,1,0:T(8,128)(2,1)S(1)}, bf16[4,2,8,1024]{3,2,1,0:T(8,128)(2,1)S(1)}, u32[]{:S(2)}, u32[]{:S(2)}) collective-permute-start(bf16[4,2,8,1024]{3,2,1,0:T(8,128)(2,1)S(1)} %get-tuple-element.26), channel_id=1, source_target_pairs={{0,2},{1,3},{2,4},{3,5},{4,6},{5,7},{6,8},{7,9},{8,10},{9,11},{10,... | collective-permute-start | bytes 393224 | tf_op jit(solution)/shard_map/ppermute | solution.py:32
  159.7 5.2 %collective-permute-start.27 = (bf16[4,2,8,1024]{3,2,1,0:T(8,128)(2,1)S(1)}, bf16[4,2,8,1024]{3,2,1,0:T(8,128)(2,1)S(1)}, u32[]{:S(2)}, u32[]{:S(2)}) collective-permute-start(bf16[4,2,8,1024]{3,2,1,0:T(8,128)(2,1)S(1)} %get-tuple-element.26), channel_id=1, source_target_pairs={{0,62},{1,63},{2,0},{3,1},{4,2},{5,3},{6,4},{7,5},{8,6},{9,7},{10,... | collective-permute-start | bytes 393224 | tf_op jit(solution)/shard_map/ppermute | solution.py:32
  165.0 3.4 %copy-start.2 = (bf16[4,4,2,8,1024]{4,3,2,1,0:T(8,128)(2,1)}, bf16[4,4,2,8,1024]{4,3,2,1,0:T(8,128)(2,1)S(1)}, u32[]{:S(2)}) copy-start(bf16[4,4,2,8,1024]{4,3,2,1,0:T(8,128)(2,1)S(1)} %pad_maximum_fusion.1) | copy-start | bytes 1572868
  165.0 3.3 %collective-permute-start.28 = (bf16[4,4,2,8,1024]{4,3,2,1,0:T(8,128)(2,1)S(1)}, bf16[4,4,2,8,1024]{4,3,2,1,0:T(8,128)(2,1)S(1)}, u32[]{:S(2)}, u32[]{:S(2)}) collective-permute-start(bf16[4,4,2,8,1024]{4,3,2,1,0:T(8,128)(2,1)S(1)} %pad_maximum_fusion.1), channel_id=1, source_target_pairs={{0,1},{1,0},{2,3},{3,2},{4,5},{5,4},{6,7},{7,6},{8,9},{9,8},{10,11... | collective-permute-start | bytes 1572872 | tf_op jit(solution)/shard_map/ppermute | solution.py:44
  168.4 0.8 copy-start.4

commit v4 on v3

--- a/solution.py
+++ b/solution.py
@@ -203,7 +203,7 @@
                 dense[active[g, q * SHARE + j], rows, :] = tile[:, j * BLK : (j + 1) * BLK]
 
     total = stream_t[...]
-    per = 4
+    per = 8
     for k in range(dense.shape[0] // per):
         if k * per * BLK % cols == 0:
             copies[k * per * BLK // cols].wait()

time: 177 us -> 177 us (level)
  no operation moved by 1% of the time
where the time goes in v4:
time: 177 us; the launch traced here: 176 us
  waiting for transfers between devices  87.6 us (49%)
  starting transfers between devices  56.4 us (32%)
  Pallas kernels  17.4 us (10%)
  local copies, waits for them, and re-layouts  5.91 us (3%)
  other arithmetic  4.52 us (3%)
  matrix products  3.59 us (2%)
    ppermute x24, waiting for transfers between devices, along_z(): return lax.ppermute(x, AXES, pairs)  81.8 us
    ppermute x24, starting transfers between devices, along_z(): return lax.ppermute(x, AXES, pairs)  33.3 us
    ppermute x5, starting transfers between devices, other_core(): return lax.ppermute(x, 'core', [(0, 1), (1, 0)])  23.1 us
    pallas_call x1, Pallas kernels, body(): pl.pallas_call(up_kernel, in_specs=[SMEM, SMEM, VMEM, VMEM, VMEM, VMEM, V...  10.9 us
    pallas_call x1, Pallas kernels, body(): pl.pallas_call(down_kernel, in_specs=[SMEM, SMEM, VMEM, VMEM, VMEM, HBM],...  6.45 us
    ppermute x5, waiting for transfers between devices, other_core(): return lax.ppermute(x, 'core', [(0, 1), (1, 0)])  5.86 us
  transfers between devices with their start and end apart: 29, of which 20 were waited for; matrix products, arithmetic and copies ran while one was open for 2% of the time, Pallas kernels for 0%

profile of v4, /device:TPU:37, one launch (start us, length us, event | category | flops | bytes accessed | tf_op | source)
XLA Modules:
  0.0 175.8 jit_solution(15476195468720534784)
XLA Ops:
  0.0 0.9 dynamic_slice.7
  1.0 0.6 copy-done
  1.6 1.6 fusion.29
  3.2 2.0 %convolution_convert_fusion = bf16[8,8,128]{2,1,0:T(8,128)(2,1)S(1)} fusion(bf16[8,1024,128]{2,1,0:T(8,128)(2,1)} %param.14, f32[8,8,1024]{2,1,0:T(8,128)S(1)} %get-tuple-element.34, f32[8,8]{1,0:T(8,128)S(1)} %get-tuple-element.33), kind=kOutput, calls=%fused_computation.7 | convolution fusion | flops 16916480 | bytes 2375936 | tf_op jit(solution)/shard_map/egt,etc->egc/dot_general | solution.py:113
  5.2 20.5 %collective-permute-start = (bf16[8,1024]{1,0:T(8,128)(2,1)S(1)}, bf16[8,1024]{1,0:T(8,128)(2,1)S(1)}, u32[]{:S(2)}, u32[]{:S(2)}) collective-permute-start(bf16[8,1024]{1,0:T(8,128)(2,1)S(1)} %bitcast.186), channel_id=1, source_target_pairs={{0,1},{1,0},{2,3},{3,2},{4,5},{5,4},{6,7},{7,6},{8,9},{9,8},{10,11... | collective-permute-start | bytes 49160 | tf_op jit(solution)/shard_map/ppermute | solution.py:44
  25.8 0.5 bitcast_convert_fusion.gain
  26.6 1.3 dynamic-slice_bitcast_fusion.order
  27.9 5.4 %collective-permute-done.1 = bf16[2,8,1024]{2,1,0:T(8,128)(2,1)S(1)} collective-permute-done((bf16[2,8,1024]{2,1,0:T(8,128)(2,1)S(1)}, bf16[2,8,1024]{2,1,0:T(8,128)(2,1)S(1)}, u32[]{:S(2)}, u32[]{:S(2)}) %collective-permute-start.1) | collective-permute-done | bytes 32800 | tf_op jit(solution)/shard_map/ppermute | solution.py:32
  33.3 6.8 %collective-permute-done.2 = bf16[2,8,1024]{2,1,0:T(8,128)(2,1)S(1)} collective-permute-done((bf16[2,8,1024]{2,1,0:T(8,128)(2,1)S(1)}, bf16[2,8,1024]{2,1,0:T(8,128)(2,1)S(1)}, u32[]{:S(2)}, u32[]{:S(2)}) %collective-permute-start.2) | collective-permute-done | bytes 32800 | tf_op jit(solution)/shard_map/ppermute | solution.py:32
  40.1 6.8 %collective-permute-done.3 = bf16[2,8,1024]{2,1,0:T(8,128)(2,1)S(1)} collective-permute-done((bf16[2,8,1024]{2,1,0:T(8,128)(2,1)S(1)}, bf16[2,8,1024]{2,1,0:T(8,128)(2,1)S(1)}, u32[]{:S(2)}, u32[]{:S(2)}) %collective-permute-start.3) | collective-permute-done | bytes 32800 | tf_op jit(solution)/shard_map/ppermute | solution.py:32
  46.8 1.9 %collective-permute-start.4 = (bf16[2,8,1024]{2,1,0:T(8,128)(2,1)S(1)}, bf16[2,8,1024]{2,1,0:T(8,128)(2,1)S(1)}, u32[]{:S(2)}, u32[]{:S(2)}) collective-permute-start(bf16[2,8,1024]{2,1,0:T(8,128)(2,1)S(1)} %collective-permute-done.3), channel_id=1, source_target_pairs={{1,9},{3,11},{5,13},{7,15},{9,17},{11,19},{13,21},{15,23},{17,25},... | collective-permute-start | bytes 98312 | tf_op jit(solution)/shard_map/ppermute | solution.py:32
  48.8 2.7 %collective-permute-start.6 = (bf16[2,2,8,1024]{3,2,1,0:T(8,128)(2,1)S(1)}, bf16[2,2,8,1024]{3,2,1,0:T(8,128)(2,1)S(1)}, u32[]{:S(2)}, u32[]{:S(2)}) collective-permute-start(bf16[2,2,8,1024]{3,2,1,0:T(8,128)(2,1)S(1)} %get-tuple-element.31), channel_id=1, source_target_pairs={{0,60},{1,5},{2,62},{3,7},{4,0},{5,9},{6,2},{7,11},{8,4},{9,13},{1... | collective-permute-start | bytes 196616 | tf_op jit(solution)/shard_map/ppermute | solution.py:32
  51.5 3.3 %collective-permute-start.7 = (bf16[2,2,8,1024]{3,2,1,0:T(8,128)(2,1)S(1)}, bf16[2,2,8,1024]{3,2,1,0:T(8,128)(2,1)S(1)}, u32[]{:S(2)}, u32[]{:S(2)}) collective-permute-start(bf16[2,2,8,1024]{3,2,1,0:T(8,128)(2,1)S(1)} %get-tuple-element.32), channel_id=1, source_target_pairs={{0,4},{1,61},{2,6},{3,63},{4,8},{5,1},{6,10},{7,3},{8,12},{9,5},{1... | collective-permute-start | bytes 196616 | tf_op jit(solution)/shard_map/ppermute | solution.py:32
  54.8 0.6 collective-permute-done.4
  55.5 1.6 collective-permute-start.5
  57.1 5.2 %collective-permute-start.8 = (bf16[4,2,8,1024]{3,2,1,0:T(8,128)(2,1)S(1)}, bf16[4,2,8,1024]{3,2,1,0:T(8,128)(2,1)S(1)}, u32[]{:S(2)}, u32[]{:S(2)}) collective-permute-start(bf16[4,2,8,1024]{3,2,1,0:T(8,128)(2,1)S(1)} %get-tuple-element.28), channel_id=1, source_target_pairs={{0,62},{1,63},{2,0},{3,1},{4,2},{5,3},{6,4},{7,5},{8,6},{9,7},{10,... | collective-permute-start | bytes 393224 | tf_op jit(solution)/shard_map/ppermute | solution.py:32
  62.3 2.2 %collective-permute-done.5 = bf16[4,2,8,1024]{3,2,1,0:T(8,128)(2,1)S(1)} collective-permute-done((bf16[4,2,8,1024]{3,2,1,0:T(8,128)(2,1)S(1)}, bf16[4,2,8,1024]{3,2,1,0:T(8,128)(2,1)S(1)}, u32[]{:S(2)}, u32[]{:S(2)}) %collective-permute-start.5) | collective-permute-done | bytes 131104 | tf_op jit(solution)/shard_map/ppermute | solution.py:32
  64.8 0.7 copy.13.residual
  65.5 1.1 collective-permute-done.9
  66.7 0.8 copy-done.3
  67.5 10.9 %up_kernel.1 = (f32[128,64]{1,0:T(8,128)}, f32[32,8,2176]{2,1,0:T(8,128)}, bf16[32,8,2176]{2,1,0:T(8,128)(2,1)}) custom-call(s32[2,64]{1,0:T(2,128)} %dynamic-slice_bitcast_fusion.order, s32[16,32]{1,0:T(8,128)} %active.3, bf16[32,8,1024]{2,1,0:T(8,128)(2,1)} %bitcast.160, bf16[32,8,1024]{2,1,0:T(8,128)(2,1)} %bitcast.164, bf16[128,64]{1,0:T(8,128)(2,1)} %copy.13.residual, ...), custom_call_target="tpu_custom_call" | custom-call | tf_op jit(solution)/shard_map/up_kernel/pallas_call | solution.py:250
  78.9 2.8 %collective-permute-done.10 = bf16[4,4,2,8,2176]{4,3,2,1,0:T(8,128)(2,1)S(1)} collective-permute-done((bf16[4,4,2,8,2176]{4,3,2,1,0:T(8,128)(2,1)}, bf16[4,4,2,8,2176]{4,3,2,1,0:T(8,128)(2,1)S(1)}, u32[]{:S(2)}, u32[]{:S(2)}) %collective-permute-start.10) | collective-permute-done | bytes 1114144 | tf_op jit(solution)/shard_map/ppermute | solution.py:44
  81.7 1.9 %fusion.28 = (bf16[4,4,2,8,2176]{4,3,2,1,0:T(8,128)(2,1)S(1)}, f32[4,4,2,8,2176]{4,3,2,1,0:T(8,128)S(1)}) fusion(f32[4,4,2,8,2176]{4,3,2,1,0:T(8,128)} %bitcast.159, bf16[4,4,2,8,2176]{4,3,2,1,0:T(8,128)(2,1)S(1)} %collective-permute-done.10), kind=kLoop, calls=%fused_computation.74 | loop fusion | flops 1671168 | bytes 6684672 | tf_op jit(solution)/shard_map/convert_element_type | solution.py:86
  83.8 2.9 %collective-permute-start.12 = (bf16[4,2,8,2176]{3,2,1,0:T(8,128)(2,1)S(1)}, bf16[4,2,8,2176]{3,2,1,0:T(8,128)(2,1)S(1)}, u32[]{:S(2)}, u32[]{:S(2)}) collective-permute-start(bf16[4,2,8,2176]{3,2,1,0:T(8,128)(2,1)S(1)} %get-tuple-element.24), channel_id=1, source_target_pairs={{0,62},{1,63},{2,0},{3,1},{4,2},{5,3},{6,4},{7,5},{8,6},{9,7},{10,... | collective-permute-start | bytes 835592 | tf_op jit(solution)/shard_map/ppermute | solution.py:32
  86.9 6.5 %collective-permute-done.11 = bf16[4,2,8,2176]{3,2,1,0:T(8,128)(2,1)S(1)} collective-permute-done((bf16[4,2,8,2176]{3,2,1,0:T(8,128)(2,1)S(1)}, bf16[4,2,8,2176]{3,2,1,0:T(8,128)(2,1)S(1)}, u32[]{:S(2)}, u32[]{:S(2)}) %collective-permute-start.11) | collective-permute-done | bytes 278560 | tf_op jit(solution)/shard_map/ppermute | solution.py:32
  93.4 2.7 %collective-permute-start.13 = (bf16[2,8,2176]{2,1,0:T(8,128)(2,1)S(1)}, bf16[2,8,2176]{2,1,0:T(8,128)(2,1)S(1)}, u32[]{:S(2)}, u32[]{:S(2)}) collective-permute-start(bf16[2,8,2176]{2,1,0:T(8,128)(2,1)S(1)} %fusion.25), channel_id=1, source_target_pairs={{1,9},{3,11},{5,13},{7,15},{9,17},{11,19},{13,21},{15,23},{17,25},... | collective-permute-start | bytes 208904 | tf_op jit(solution)/shard_map/ppermute | solution.py:32
  96.1 2.3 %collective-permute-start.16 = (bf16[2,2,8,2176]{3,2,1,0:T(8,128)(2,1)S(1)}, bf16[2,2,8,2176]{3,2,1,0:T(8,128)(2,1)S(1)}, u32[]{:S(2)}, u32[]{:S(2)}) collective-permute-start(bf16[2,2,8,2176]{3,2,1,0:T(8,128)(2,1)S(1)} %get-tuple-element.21), channel_id=1, source_target_pairs={{0,4},{1,61},{2,6},{3,63},{4,8},{5,1},{6,10},{7,3},{8,12},{9,5},{1... | collective-permute-start | bytes 417800 | tf_op jit(solution)/shard_map/ppermute | solution.py:32
  98.4 7.2 %collective-permute-done.13 = bf16[2,8,2176]{2,1,0:T(8,128)(2,1)S(1)} collective-permute-done((bf16[2,8,2176]{2,1,0:T(8,128)(2,1)S(1)}, bf16[2,8,2176]{2,1,0:T(8,128)(2,1)S(1)}, u32[]{:S(2)}, u32[]{:S(2)}) %collective-permute-start.13) | collective-permute-done | bytes 69664 | tf_op jit(solution)/shard_map/ppermute | solution.py:32
  105.8 7.3 %collective-permute-done.15 = bf16[2,8,2176]{2,1,0:T(8,128)(2,1)S(1)} collective-permute-done((bf16[2,8,2176]{2,1,0:T(8,128)(2,1)S(1)}, bf16[2,8,2176]{2,1,0:T(8,128)(2,1)S(1)}, u32[]{:S(2)}, u32[]{:S(2)}) %collective-permute-start.15) | collective-permute-done | bytes 69664 | tf_op jit(solution)/shard_map/ppermute | solution.py:32
  113.2 7.1 %collective-permute-done.17 = bf16[2,8,2176]{2,1,0:T(8,128)(2,1)S(1)} collective-permute-done((bf16[2,8,2176]{2,1,0:T(8,128)(2,1)S(1)}, bf16[2,8,2176]{2,1,0:T(8,128)(2,1)S(1)}, u32[]{:S(2)}, u32[]{:S(2)}) %collective-permute-start.17) | collective-permute-done | bytes 69664 | tf_op jit(solution)/shard_map/ppermute | solution.py:32
  120.5 7.1 %collective-permute-done.18 = bf16[2,8,2176]{2,1,0:T(8,128)(2,1)S(1)} collective-permute-done((bf16[2,8,2176]{2,1,0:T(8,128)(2,1)S(1)}, bf16[2,8,2176]{2,1,0:T(8,128)(2,1)S(1)}, u32[]{:S(2)}, u32[]{:S(2)}) %collective-permute-start.18) | collective-permute-done | bytes 69664 | tf_op jit(solution)/shard_map/ppermute | solution.py:32
  127.7 0.6 add_reduce_fusion
  128.3 0.7 collective-permute-done.19
  129.1 0.7 add_divide_fusion
  130.0 6.6 %collective-permute-done.20 = bf16[2,8,1024]{2,1,0:T(8,128)(2,1)S(1)} collective-permute-done((bf16[2,8,1024]{2,1,0:T(8,128)(2,1)S(1)}, bf16[2,8,1024]{2,1,0:T(8,128)(2,1)S(1)}, u32[]{:S(2)}, u32[]{:S(2)}) %collective-permute-start.20) | collective-permute-done | bytes 32800 | tf_op jit(solution)/shard_map/ppermute | solution.py:32
  136.7 6.6 %collective-permute-done.21 = bf16[2,8,1024]{2,1,0:T(8,128)(2,1)S(1)} collective-permute-done((bf16[2,8,1024]{2,1,0:T(8,128)(2,1)S(1)}, bf16[2,8,1024]{2,1,0:T(8,128)(2,1)S(1)}, u32[]{:S(2)}, u32[]{:S(2)}) %collective-permute-start.21) | collective-permute-done | bytes 32800 | tf_op jit(solution)/shard_map/ppermute | solution.py:32
  143.3 6.6 %collective-permute-done.22 = bf16[2,8,1024]{2,1,0:T(8,128)(2,1)S(1)} collective-permute-done((bf16[2,8,1024]{2,1,0:T(8,128)(2,1)S(1)}, bf16[2,8,1024]{2,1,0:T(8,128)(2,1)S(1)}, u32[]{:S(2)}, u32[]{:S(2)}) %collective-permute-start.22) | collective-permute-done | bytes 32800 | tf_op jit(solution)/shard_map/ppermute | solution.py:32
  150.0 2.0 %collective-permute-start.23 = (bf16[2,8,1024]{2,1,0:T(8,128)(2,1)S(1)}, bf16[2,8,1024]{2,1,0:T(8,128)(2,1)S(1)}, u32[]{:S(2)}, u32[]{:S(2)}) collective-permute-start(bf16[2,8,1024]{2,1,0:T(8,128)(2,1)S(1)} %collective-permute-done.22), channel_id=1, source_target_pairs={{1,9},{3,11},{5,13},{7,15},{9,17},{11,19},{13,21},{15,23},{17,25},... | collective-permute-start | bytes 98312 | tf_op jit(solution)/shard_map/ppermute | solution.py:32
  152.0 4.9 %collective-permute-start.25 = (bf16[2,2,8,1024]{3,2,1,0:T(8,128)(2,1)S(1)}, bf16[2,2,8,1024]{3,2,1,0:T(8,128)(2,1)S(1)}, u32[]{:S(2)}, u32[]{:S(2)}) collective-permute-start(bf16[2,2,8,1024]{3,2,1,0:T(8,128)(2,1)S(1)} %get-tuple-element.29), channel_id=1, source_target_pairs={{0,60},{1,5},{2,62},{3,7},{4,0},{5,9},{6,2},{7,11},{8,4},{9,13},{1... | collective-permute-start | bytes 196616 | tf_op jit(solution)/shard_map/ppermute | solution.py:32
  156.9 1.7 collective-permute-done.23
  158.6 1.1 collective-permute-start.24
  159.7 1.7 collective-permute-start.27
  161.5 3.5 %collective-permute-done.24 = bf16[4,2,8,1024]{3,2,1,0:T(8,128)(2,1)S(1)} collective-permute-done((bf16[4,2,8,1024]{3,2,1,0:T(8,128)(2,1)S(1)}, bf16[4,2,8,1024]{3,2,1,0:T(8,128)(2,1)S(1)}, u32[]{:S(2)}, u32[]{:S(2)}) %collective-permute-start.24) | collective-permute-done | bytes 131104 | tf_op jit(solution)/shard_map/ppermute | solution.py:32
  165.0 1.8 %collective-permute-start.28 = (bf16[4,4,2,8,1024]{4,3,2,1,0:T(8,128)(2,1)S(1)}, bf16[4,4,2,8,1024]{4,3,2,1,0:T(8,128)(2,1)S(1)}, u32[]{:S(2)}, u32[]{:S(2)}) collective-permute-start(bf16[4,4,2,8,1024]{4,3,2,1,0:T(8,128)(2,1)S(1)} %pad_maximum_fusion.1), channel_id=1, source_target_pairs={{0,1},{1,0},{2,3},{3,2},{4,5},{5,4},{6,7},{7,6},{8,9},{9,8},{10,11... | collective-permute-start | bytes 1572872 | tf_op jit(solution)/shard_map/ppermute | solution.py:44
  166.9 0.7 copy.14
  167.5 0.8 collective-permute-done.28
  168.4 0.8 copy-done.4
  169.2 6.4 %down_kernel.1 = bf16[64,128]{1,0:T(8,128)(2,1)} custom-call(s32[2,64]{1,0:T(2,128)} %dynamic-slice_bitcast_fusion.order, s32[16,32]{1,0:T(8,128)} %active.3, bf16[32,8,1024]{2,1,0:T(8,128)(2,1)} %bitcast.161, bf16[32,8,1024]{2,1,0:T(8,128)(2,1)} %bitcast.165, f32[64,128]{1,0:T(8,128)} %bitcast.167, bf16[64,14336]{1,0:T(8,128)(2,1)} %bitcast.162), custom_call_target="tpu_custom_call" | custom-call | tf_op jit(solution)/shard_map/down_kernel/pallas_call | solution.py:290
  (62 shorter events, 2.9 us)
Async XLA Ops:
  0.0 1.6 copy-start
  1.6 24.2 %copy-start.7 = (bf16[64]{0:T(256)(128)(2,1)S(1)}, bf16[64]{0:T(256)(128)(2,1)}, u32[]{:S(2)}) copy-start(bf16[64]{0:T(256)(128)(2,1)} %param.19) | copy-start | bytes 388
  3.2 61.6 %copy-start.6 = (bf16[128,64]{0,1:T(8,128)(2,1)S(1)}, bf16[128,64]{0,1:T(8,128)(2,1)}, u32[]{:S(2)}) copy-start(bf16[128,64]{0,1:T(8,128)(2,1)} %param.17) | copy-start | bytes 49156
  5.2 21.4 %collective-permute-start = (bf16[8,1024]{1,0:T(8,128)(2,1)S(1)}, bf16[8,1024]{1,0:T(8,128)(2,1)S(1)}, u32[]{:S(2)}, u32[]{:S(2)}) collective-permute-start(bf16[8,1024]{1,0:T(8,128)(2,1)S(1)} %bitcast.186), channel_id=1, source_target_pairs={{0,1},{1,0},{2,3},{3,2},{4,5},{5,4},{6,7},{7,6},{8,9},{9,8},{10,11... | collective-permute-start | bytes 49160 | tf_op jit(solution)/shard_map/ppermute | solution.py:44
  26.6 6.7 %collective-permute-start.1 = (bf16[2,8,1024]{2,1,0:T(8,128)(2,1)S(1)}, bf16[2,8,1024]{2,1,0:T(8,128)(2,1)S(1)}, u32[]{:S(2)}, u32[]{:S(2)}) collective-permute-start(bf16[2,8,1024]{2,1,0:T(8,128)(2,1)S(1)} %pad_maximum_fusion.8), channel_id=1, source_target_pairs={{0,56},{1,9},{2,58},{3,11},{4,60},{5,13},{6,62},{7,15},{8,0},{9,17... | collective-permute-start | bytes 98312 | tf_op jit(solution)/shard_map/ppermute | solution.py:32
  33.3 6.8 %collective-permute-start.2 = (bf16[2,8,1024]{2,1,0:T(8,128)(2,1)S(1)}, bf16[2,8,1024]{2,1,0:T(8,128)(2,1)S(1)}, u32[]{:S(2)}, u32[]{:S(2)}) collective-permute-start(bf16[2,8,1024]{2,1,0:T(8,128)(2,1)S(1)} %collective-permute-done.1), channel_id=1, source_target_pairs={{0,56},{1,9},{2,58},{3,11},{4,60},{5,13},{6,62},{7,15},{8,0},{9,17... | collective-permute-start | bytes 98312 | tf_op jit(solution)/shard_map/ppermute | solution.py:32
  40.1 6.8 %collective-permute-start.3 = (bf16[2,8,1024]{2,1,0:T(8,128)(2,1)S(1)}, bf16[2,8,1024]{2,1,0:T(8,128)(2,1)S(1)}, u32[]{:S(2)}, u32[]{:S(2)}) collective-permute-start(bf16[2,8,1024]{2,1,0:T(8,128)(2,1)S(1)} %collective-permute-done.2), channel_id=1, source_target_pairs={{0,56},{1,9},{2,58},{3,11},{4,60},{5,13},{6,62},{7,15},{8,0},{9,17... | collective-permute-start | bytes 98312 | tf_op jit(solution)/shard_map/ppermute | solution.py:32
  46.8 8.6 %collective-permute-start.4 = (bf16[2,8,1024]{2,1,0:T(8,128)(2,1)S(1)}, bf16[2,8,1024]{2,1,0:T(8,128)(2,1)S(1)}, u32[]{:S(2)}, u32[]{:S(2)}) collective-permute-start(bf16[2,8,1024]{2,1,0:T(8,128)(2,1)S(1)} %collective-permute-done.3), channel_id=1, source_target_pairs={{1,9},{3,11},{5,13},{7,15},{9,17},{11,19},{13,21},{15,23},{17,25},... | collective-permute-start | bytes 98312 | tf_op jit(solution)/shard_map/ppermute | solution.py:32
  48.8 13.5 %collective-permute-start.6 = (bf16[2,2,8,1024]{3,2,1,0:T(8,128)(2,1)S(1)}, bf16[2,2,8,1024]{3,2,1,0:T(8,128)(2,1)S(1)}, u32[]{:S(2)}, u32[]{:S(2)}) collective-permute-start(bf16[2,2,8,1024]{3,2,1,0:T(8,128)(2,1)S(1)} %get-tuple-element.31), channel_id=1, source_target_pairs={{0,60},{1,5},{2,62},{3,7},{4,0},{5,9},{6,2},{7,11},{8,4},{9,13},{1... | collective-permute-start | bytes 196616 | tf_op jit(solution)/shard_map/ppermute | solution.py:32
  51.5 10.8 %collective-permute-start.7 = (bf16[2,2,8,1024]{3,2,1,0:T(8,128)(2,1)S(1)}, bf16[2,2,8,1024]{3,2,1,0:T(8,128)(2,1)S(1)}, u32[]{:S(2)}, u32[]{:S(2)}) collective-permute-start(bf16[2,2,8,1024]{3,2,1,0:T(8,128)(2,1)S(1)} %get-tuple-element.32), channel_id=1, source_target_pairs={{0,4},{1,61},{2,6},{3,63},{4,8},{5,1},{6,10},{7,3},{8,12},{9,5},{1... | collective-permute-start | bytes 196616 | tf_op jit(solution)/shard_map/ppermute | solution.py:32
  55.5 9.1 %collective-permute-start.5 = (bf16[4,2,8,1024]{3,2,1,0:T(8,128)(2,1)S(1)}, bf16[4,2,8,1024]{3,2,1,0:T(8,128)(2,1)S(1)}, u32[]{:S(2)}, u32[]{:S(2)}) collective-permute-start(bf16[4,2,8,1024]{3,2,1,0:T(8,128)(2,1)S(1)} %get-tuple-element.28), channel_id=1, source_target_pairs={{0,2},{1,3},{2,4},{3,5},{4,6},{5,7},{6,8},{7,9},{8,10},{9,11},{10,... | collective-permute-start | bytes 393224 | tf_op jit(solution)/shard_map/ppermute | solution.py:32
  57.1 7.4 %collective-permute-start.8 = (bf16[4,2,8,1024]{3,2,1,0:T(8,128)(2,1)S(1)}, bf16[4,2,8,1024]{3,2,1,0:T(8,128)(2,1)S(1)}, u32[]{:S(2)}, u32[]{:S(2)}) collective-permute-start(bf16[4,2,8,1024]{3,2,1,0:T(8,128)(2,1)S(1)} %get-tuple-element.28), channel_id=1, source_target_pairs={{0,62},{1,63},{2,0},{3,1},{4,2},{5,3},{6,4},{7,5},{8,6},{9,7},{10,... | collective-permute-start | bytes 393224 | tf_op jit(solution)/shard_map/ppermute | solution.py:32
  64.6 2.0 %copy-start.1 = (bf16[4,4,2,8,1024]{4,3,2,1,0:T(8,128)(2,1)}, bf16[4,4,2,8,1024]{4,3,2,1,0:T(8,128)(2,1)S(1)}, u32[]{:S(2)}) copy-start(bf16[4,4,2,8,1024]{4,3,2,1,0:T(8,128)(2,1)S(1)} %pad_maximum_fusion) | copy-start | bytes 1572868
  64.6 2.0 %collective-permute-start.9 = (bf16[4,4,2,8,1024]{4,3,2,1,0:T(8,128)(2,1)S(1)}, bf16[4,4,2,8,1024]{4,3,2,1,0:T(8,128)(2,1)S(1)}, u32[]{:S(2)}, u32[]{:S(2)}) collective-permute-start(bf16[4,4,2,8,1024]{4,3,2,1,0:T(8,128)(2,1)S(1)} %pad_maximum_fusion), channel_id=1, source_target_pairs={{0,1},{1,0},{2,3},{3,2},{4,5},{5,4},{6,7},{7,6},{8,9},{9,8},{10,11... | collective-permute-start | bytes 1572872 | tf_op jit(solution)/shard_map/ppermute | solution.py:44
  66.7 0.8 copy-start.3
  78.4 3.3 %collective-permute-start.10 = (bf16[4,4,2,8,2176]{4,3,2,1,0:T(8,128)(2,1)}, bf16[4,4,2,8,2176]{4,3,2,1,0:T(8,128)(2,1)S(1)}, u32[]{:S(2)}, u32[]{:S(2)}) collective-permute-start(bf16[4,4,2,8,2176]{4,3,2,1,0:T(8,128)(2,1)} %bitcast.187), channel_id=1, source_target_pairs={{0,1},{1,0},{2,3},{3,2},{4,5},{5,4},{6,7},{7,6},{8,9},{9,8},{10,11... | collective-permute-start | bytes 3342344 | tf_op jit(solution)/shard_map/ppermute | solution.py:44
  83.7 9.7 %collective-permute-start.11 = (bf16[4,2,8,2176]{3,2,1,0:T(8,128)(2,1)S(1)}, bf16[4,2,8,2176]{3,2,1,0:T(8,128)(2,1)S(1)}, u32[]{:S(2)}, u32[]{:S(2)}) collective-permute-start(bf16[4,2,8,2176]{3,2,1,0:T(8,128)(2,1)S(1)} %get-tuple-element.23), channel_id=1, source_target_pairs={{0,2},{1,3},{2,4},{3,5},{4,6},{5,7},{6,8},{7,9},{8,10},{9,11},{10,... | collective-permute-start | bytes 835592 | tf_op jit(solution)/shard_map/ppermute | solution.py:32
  83.8 9.5 %collective-permute-start.12 = (bf16[4,2,8,2176]{3,2,1,0:T(8,128)(2,1)S(1)}, bf16[4,2,8,2176]{3,2,1,0:T(8,128)(2,1)S(1)}, u32[]{:S(2)}, u32[]{:S(2)}) collective-permute-start(bf16[4,2,8,2176]{3,2,1,0:T(8,128)(2,1)S(1)} %get-tuple-element.24), channel_id=1, source_target_pairs={{0,62},{1,63},{2,0},{3,1},{4,2},{5,3},{6,4},{7,5},{8,6},{9,7},{10,... | collective-permute-start | bytes 835592 | tf_op jit(solution)/shard_map/ppermute | solution.py:32
  86.8 11.6 %collective-permute-start.14 = (bf16[2,2,8,2176]{3,2,1,0:T(8,128)(2,1)S(1)}, bf16[2,2,8,2176]{3,2,1,0:T(8,128)(2,1)S(1)}, u32[]{:S(2)}, u32[]{:S(2)}) collective-permute-start(bf16[2,2,8,2176]{3,2,1,0:T(8,128)(2,1)S(1)} %get-tuple-element.22), channel_id=1, source_target_pairs={{0,60},{1,5},{2,62},{3,7},{4,0},{5,9},{6,2},{7,11},{8,4},{9,13},{1... | collective-permute-start | bytes 417800 | tf_op jit(solution)/shard_map/ppermute | solution.py:32
  93.4 12.2 %collective-permute-start.13 = (bf16[2,8,2176]{2,1,0:T(8,128)(2,1)S(1)}, bf16[2,8,2176]{2,1,0:T(8,128)(2,1)S(1)}, u32[]{:S(2)}, u32[]{:S(2)}) collective-permute-start(bf16[2,8,2176]{2,1,0:T(8,128)(2,1)S(1)} %fusion.25), channel_id=1, source_target_pairs={{1,9},{3,11},{5,13},{7,15},{9,17},{11,19},{13,21},{15,23},{17,25},... | collective-permute-start | bytes 208904 | tf_op jit(solution)/shard_map/ppermute | solution.py:32
  96.1 9.7 %collective-permute-start.16 = (bf16[2,2,8,2176]{3,2,1,0:T(8,128)(2,1)S(1)}, bf16[2,2,8,2176]{3,2,1,0:T(8,128)(2,1)S(1)}, u32[]{:S(2)}, u32[]{:S(2)}) collective-permute-start(bf16[2,2,8,2176]{3,2,1,0:T(8,128)(2,1)S(1)} %get-tuple-element.21), channel_id=1, source_target_pairs={{0,4},{1,61},{2,6},{3,63},{4,8},{5,1},{6,10},{7,3},{8,12},{9,5},{1... | collective-permute-start | bytes 417800 | tf_op jit(solution)/shard_map/ppermute | solution.py:32
  105.6 61.3 %copy-start.5 = (f32[128,64]{1,0:T(8,128)S(1)}, f32[128,64]{1,0:T(8,128)}, u32[]{:S(2)}) copy-start(f32[128,64]{1,0:T(8,128)} %get-tuple-element.18) | copy-start | bytes 98308
  105.6 7.4 %collective-permute-start.15 = (bf16[2,8,2176]{2,1,0:T(8,128)(2,1)S(1)}, bf16[2,8,2176]{2,1,0:T(8,128)(2,1)S(1)}, u32[]{:S(2)}, u32[]{:S(2)}) collective-permute-start(bf16[2,8,2176]{2,1,0:T(8,128)(2,1)S(1)} %fusion.19), channel_id=1, source_target_pairs={{0,56},{1,9},{2,58},{3,11},{4,60},{5,13},{6,62},{7,15},{8,0},{9,17... | collective-permute-start | bytes 208904 | tf_op jit(solution)/shard_map/ppermute | solution.py:32
  113.1 7.2 %collective-permute-start.17 = (bf16[2,8,2176]{2,1,0:T(8,128)(2,1)S(1)}, bf16[2,8,2176]{2,1,0:T(8,128)(2,1)S(1)}, u32[]{:S(2)}, u32[]{:S(2)}) collective-permute-start(bf16[2,8,2176]{2,1,0:T(8,128)(2,1)S(1)} %fusion.14), channel_id=1, source_target_pairs={{0,56},{1,9},{2,58},{3,11},{4,60},{5,13},{6,62},{7,15},{8,0},{9,17... | collective-permute-start | bytes 208904 | tf_op jit(solution)/shard_map/ppermute | solution.py:32
  120.3 7.2 %collective-permute-start.18 = (bf16[2,8,2176]{2,1,0:T(8,128)(2,1)S(1)}, bf16[2,8,2176]{2,1,0:T(8,128)(2,1)S(1)}, u32[]{:S(2)}, u32[]{:S(2)}) collective-permute-start(bf16[2,8,2176]{2,1,0:T(8,128)(2,1)S(1)} %fusion.9), channel_id=1, source_target_pairs={{0,56},{1,9},{2,58},{3,11},{4,60},{5,13},{6,62},{7,15},{8,0},{9,17... | collective-permute-start | bytes 208904 | tf_op jit(solution)/shard_map/ppermute | solution.py:32
  127.5 1.5 collective-permute-start.19
  129.9 6.7 %collective-permute-start.20 = (bf16[2,8,1024]{2,1,0:T(8,128)(2,1)S(1)}, bf16[2,8,1024]{2,1,0:T(8,128)(2,1)S(1)}, u32[]{:S(2)}, u32[]{:S(2)}) collective-permute-start(bf16[2,8,1024]{2,1,0:T(8,128)(2,1)S(1)} %fusion.24), channel_id=1, source_target_pairs={{0,56},{1,9},{2,58},{3,11},{4,60},{5,13},{6,62},{7,15},{8,0},{9,17... | collective-permute-start | bytes 98312 | tf_op jit(solution)/shard_map/ppermute | solution.py:32
  136.6 6.7 %collective-permute-start.21 = (bf16[2,8,1024]{2,1,0:T(8,128)(2,1)S(1)}, bf16[2,8,1024]{2,1,0:T(8,128)(2,1)S(1)}, u32[]{:S(2)}, u32[]{:S(2)}) collective-permute-start(bf16[2,8,1024]{2,1,0:T(8,128)(2,1)S(1)} %collective-permute-done.20), channel_id=1, source_target_pairs={{0,56},{1,9},{2,58},{3,11},{4,60},{5,13},{6,62},{7,15},{8,0},{9,17... | collective-permute-start | bytes 98312 | tf_op jit(solution)/shard_map/ppermute | solution.py:32
  143.3 6.7 %collective-permute-start.22 = (bf16[2,8,1024]{2,1,0:T(8,128)(2,1)S(1)}, bf16[2,8,1024]{2,1,0:T(8,128)(2,1)S(1)}, u32[]{:S(2)}, u32[]{:S(2)}) collective-permute-start(bf16[2,8,1024]{2,1,0:T(8,128)(2,1)S(1)} %collective-permute-done.21), channel_id=1, source_target_pairs={{0,56},{1,9},{2,58},{3,11},{4,60},{5,13},{6,62},{7,15},{8,0},{9,17... | collective-permute-start | bytes 98312 | tf_op jit(solution)/shard_map/ppermute | solution.py:32
  150.0 8.6 %collective-permute-start.23 = (bf16[2,8,1024]{2,1,0:T(8,128)(2,1)S(1)}, bf16[2,8,1024]{2,1,0:T(8,128)(2,1)S(1)}, u32[]{:S(2)}, u32[]{:S(2)}) collective-permute-start(bf16[2,8,1024]{2,1,0:T(8,128)(2,1)S(1)} %collective-permute-done.22), channel_id=1, source_target_pairs={{1,9},{3,11},{5,13},{7,15},{9,17},{11,19},{13,21},{15,23},{17,25},... | collective-permute-start | bytes 98312 | tf_op jit(solution)/shard_map/ppermute | solution.py:32
  152.0 9.5 %collective-permute-start.25 = (bf16[2,2,8,1024]{3,2,1,0:T(8,128)(2,1)S(1)}, bf16[2,2,8,1024]{3,2,1,0:T(8,128)(2,1)S(1)}, u32[]{:S(2)}, u32[]{:S(2)}) collective-permute-start(bf16[2,2,8,1024]{3,2,1,0:T(8,128)(2,1)S(1)} %get-tuple-element.29), channel_id=1, source_target_pairs={{0,60},{1,5},{2,62},{3,7},{4,0},{5,9},{6,2},{7,11},{8,4},{9,13},{1... | collective-permute-start | bytes 196616 | tf_op jit(solution)/shard_map/ppermute | solution.py:32
  156.9 4.6 %collective-permute-start.26 = (bf16[2,2,8,1024]{3,2,1,0:T(8,128)(2,1)S(1)}, bf16[2,2,8,1024]{3,2,1,0:T(8,128)(2,1)S(1)}, u32[]{:S(2)}, u32[]{:S(2)}) collective-permute-start(bf16[2,2,8,1024]{3,2,1,0:T(8,128)(2,1)S(1)} %get-tuple-element.30), channel_id=1, source_target_pairs={{0,4},{1,61},{2,6},{3,63},{4,8},{5,1},{6,10},{7,3},{8,12},{9,5},{1... | collective-permute-start | bytes 196616 | tf_op jit(solution)/shard_map/ppermute | solution.py:32
  158.6 6.3 %collective-permute-start.24 = (bf16[4,2,8,1024]{3,2,1,0:T(8,128)(2,1)S(1)}, bf16[4,2,8,1024]{3,2,1,0:T(8,128)(2,1)S(1)}, u32[]{:S(2)}, u32[]{:S(2)}) collective-permute-start(bf16[4,2,8,1024]{3,2,1,0:T(8,128)(2,1)S(1)} %get-tuple-element.26), channel_id=1, source_target_pairs={{0,2},{1,3},{2,4},{3,5},{4,6},{5,7},{6,8},{7,9},{8,10},{9,11},{10,... | collective-permute-start | bytes 393224 | tf_op jit(solution)/shard_map/ppermute | solution.py:32
  159.7 5.2 %collective-permute-start.27 = (bf16[4,2,8,1024]{3,2,1,0:T(8,128)(2,1)S(1)}, bf16[4,2,8,1024]{3,2,1,0:T(8,128)(2,1)S(1)}, u32[]{:S(2)}, u32[]{:S(2)}) collective-permute-start(bf16[4,2,8,1024]{3,2,1,0:T(8,128)(2,1)S(1)} %get-tuple-element.26), channel_id=1, source_target_pairs={{0,62},{1,63},{2,0},{3,1},{4,2},{5,3},{6,4},{7,5},{8,6},{9,7},{10,... | collective-permute-start | bytes 393224 | tf_op jit(solution)/shard_map/ppermute | solution.py:32
  165.0 3.4 %copy-start.2 = (bf16[4,4,2,8,1024]{4,3,2,1,0:T(8,128)(2,1)}, bf16[4,4,2,8,1024]{4,3,2,1,0:T(8,128)(2,1)S(1)}, u32[]{:S(2)}) copy-start(bf16[4,4,2,8,1024]{4,3,2,1,0:T(8,128)(2,1)S(1)} %pad_maximum_fusion.1) | copy-start | bytes 1572868
  165.0 3.3 %collective-permute-start.28 = (bf16[4,4,2,8,1024]{4,3,2,1,0:T(8,128)(2,1)S(1)}, bf16[4,4,2,8,1024]{4,3,2,1,0:T(8,128)(2,1)S(1)}, u32[]{:S(2)}, u32[]{:S(2)}) collective-permute-start(bf16[4,4,2,8,1024]{4,3,2,1,0:T(8,128)(2,1)S(1)} %pad_maximum_fusion.1), channel_id=1, source_target_pairs={{0,1},{1,0},{2,3},{3,2},{4,5},{5,4},{6,7},{7,6},{8,9},{9,8},{10,11... | collective-permute-start | bytes 1572872 | tf_op jit(solution)/shard_map/ppermute | solution.py:44
  168.4 0.8 copy-start.4
